TPU v7x, 1024 devices: a whole 8x8x8 slice. The times are simulated.
1024 devices in a mesh: gx: 16 (over x_hi, z), gy: 8 (over y), gz: 8 (over x_lo, core).
Axes of the slice: x: 8 (x_hi: 2, x_lo: 4; x = x_hi * 4 + x_lo), y: 8, z: 8, core: 2. Of those that a mesh axis runs over, the one named last changes fastest.
Arguments:
- displacement: float32 [3, 256, 256, 2048], P(None, 'gx', 'gy', 'gz'), may hold values from -1.5 to 1.5
- density: float32 [256, 256, 2048], P('gx', 'gy', 'gz'), may hold values from 0.03 to 1
- stiffness: float32 [24, 24], replicated, may hold values from -9 to 9.5, as said below
Outputs:
- filtered: float32 [256, 256, 2048], P('gx', 'gy', 'gz')
- compliance: float32 [], replicated
- volume: float32 [], replicated
Inputs may be any that keep to these rules, and one draw needn't show every extreme that they name: `stiffness`: symmetric and positive definite, every eigenvalue at least 0.5.
All inputs are finite; a program needn't handle non-finite values.
Results may differ from a plain program's by a relative error of at most 0.00005.
Values sent between devices are 32-bit elements; how exact they have to be, the bound alone decides.
A program may use at most 32 MiB of HBM per device.

v0:
```python
import jax
import jax.numpy as jnp
from jax import lax
from jax.sharding import Mesh
from jax.sharding import PartitionSpec as P

GX = ("gx_0", "gx_1")
GZ = ("gz_0", "gz_1")
GX_GY_GZ = ("gx_0", "gx_1", "gy", "gz_0", "gz_1")


VOID_STIFFNESS = 0.001
KERNEL = (1.0, 2.0, 3.0, 2.0, 1.0)


def from_behind(block, axis, distance):
    devices = range(lax.axis_size(axis))
    route = [(i - distance, i) for i in devices if i - distance in devices]
    return lax.ppermute(block, axis, route)


def with_halo(shard, sides, width):
    for axis, dim in sides:
        count, length = (lax.axis_size(axis), shard.shape[dim])
        up = [(i, (i + 1) % count) for i in range(count - 1)]
        down = [(j, i) for i, j in up]
        last = lax.slice_in_dim(shard, length - width, length, axis=dim)
        first = lax.slice_in_dim(shard, 0, width, axis=dim)
        before = lax.ppermute(last, axis, up)
        after = lax.ppermute(first, axis, down)
        shard = jnp.concatenate([before, shard, after], axis=dim)
    return shard


def over_axes(shard, axes):
    for axis in axes:
        shard = lax.psum(shard, axis)
    return shard


def smooth(values, along):
    length = values.shape[along] - 4
    summed = None
    for offset in range(5):
        section = lax.slice_in_dim(values, offset, offset + length, axis=along)
        scaled = KERNEL[offset] * section
        summed = scaled if summed is None else summed + scaled
    return summed


def side_sums(first, amount, extent):
    position = first + jnp.arange(amount, dtype=jnp.int32)
    summed = jnp.zeros((amount,), jnp.float32)
    for offset in range(5):
        inside = (position + offset - 2 >= 0) & (position + offset - 2 < extent)
        summed = summed + KERNEL[offset] * inside.astype(jnp.float32)
    return summed


def plane_energy(slab_nodes, stiffness):
    height = slab_nodes.shape[2] - 1
    length = slab_nodes.shape[3] - 1
    corner_rows = jnp.stack(
        [
            slab_nodes[
                member, along_x, along_y : along_y + height, along_z : along_z + length
            ].reshape(-1)
            for member in range(3)
            for along_x in range(2)
            for along_y in range(2)
            for along_z in range(2)
        ]
    )
    product = jnp.dot(
        stiffness, corner_rows, precision=lax.Precision.HIGHEST, preferred_element_type=jnp.float32
    )
    return jnp.sum(corner_rows * product, axis=0).reshape(height, length)


def energies(node_field, stiffness, planes):

    def one_plane(plane_index):
        slab_nodes = lax.dynamic_slice_in_dim(node_field, plane_index, 2, 1)
        return plane_energy(slab_nodes, stiffness)

    return lax.map(one_plane, jnp.arange(planes, dtype=jnp.int32))


def hole_sums(cells_first, cells_second, cells_third, margin):
    first_sums = side_sums(
        lax.axis_index(GX) * cells_first - margin,
        cells_first + 2 * margin,
        cells_first * lax.axis_size(GX),
    )
    second_sums = side_sums(
        lax.axis_index("gy") * cells_second - margin,
        cells_second + 2 * margin,
        cells_second * lax.axis_size("gy"),
    )
    third_sums = side_sums(
        lax.axis_index(GZ) * cells_third - margin,
        cells_third + 2 * margin,
        cells_third * lax.axis_size(GZ),
    )
    return first_sums[:, None, None] * second_sums[None, :, None] * third_sums[None, None, :]


def on_device(displacement, density, stiffness):
    cells_first, cells_second, cells_third = density.shape
    modulus = VOID_STIFFNESS + density * density * density * (1.0 - VOID_STIFFNESS)
    node_field = displacement
    upper_layer = from_behind(node_field[:, :1], GX, -1)
    node_field = jnp.concatenate([node_field, upper_layer], axis=1)
    upper_layer = from_behind(node_field[:, :, :1], "gy", -1)
    node_field = jnp.concatenate([node_field, upper_layer], axis=2)
    upper_layer = from_behind(node_field[:, :, :, :1], GZ, -1)
    node_field = jnp.concatenate([node_field, upper_layer], axis=3)
    energy = energies(node_field, stiffness, cells_first)
    sensitivity = -3.0 * (1.0 - VOID_STIFFNESS) * density * density * energy
    weighted = sensitivity / hole_sums(cells_first, cells_second, cells_third, 0)
    spread = with_halo(weighted, ((GX, 0), ("gy", 1), (GZ, 2)), 2)
    filtered = smooth(smooth(smooth(spread, 0), 1), 2)
    totals = (over_axes(jnp.sum(modulus * energy), GX_GY_GZ), over_axes(jnp.sum(density), GX_GY_GZ))
    cell_count = float(
        cells_first
        * cells_second
        * cells_third
        * lax.axis_size(GX)
        * lax.axis_size("gy")
        * lax.axis_size(GZ)
    )
    return (filtered, totals[0] / cell_count, totals[1] / cell_count)


def solution(mesh):
    finer = Mesh(
        mesh.devices.reshape(2, 8, mesh.shape["gy"], 4, 2), ("gx_0", "gx_1", "gy", "gz_0", "gz_1")
    )
    return jax.shard_map(
        on_device,
        mesh=finer,
        in_specs=(P(None, GX, "gy", GZ), P(GX, "gy", GZ), P()),
        out_specs=(P(GX, "gy", GZ), P(), P()),
        check_vma=False,
    )
```

profile of v0, /device:TPU:1, one launch (start us, length us, event | category | flops | bytes accessed | tf_op | source)
XLA Modules:
  0.0 255.5 jit_solution(13409796020747372399)
XLA Ops:
  2.8 1.5 constant_dynamic-update-slice_fusion.2
  4.4 4.9 %collective-permute-done = f32[3,1,32,256]{3,2,1,0:T(8,128)S(1)} collective-permute-done((f32[3,1,32,256]{3,2,1,0:T(8,128)S(1)}, f32[3,1,32,256]{3,2,1,0:T(8,128)S(1)}, u32[]{:S(2)}, u32[]{:S(2)}) %collective-permute-start) | collective-permute-done | bytes 98336 | tf_op jit(solution)/shard_map/ppermute | solution.py:19
  10.7 3.9 %collective-permute-done.1 = f32[3,17,1,256]{3,2,1,0:T(1,128)S(1)} collective-permute-done((f32[3,17,1,256]{3,2,1,0:T(1,128)S(1)}, f32[3,17,1,256]{3,2,1,0:T(1,128)S(1)}, u32[]{:S(2)}, u32[]{:S(2)}) %collective-permute-start.1) | collective-permute-done | bytes 52256 | tf_op jit(solution)/shard_map/ppermute | solution.py:19
  15.2 15.5 %collective-permute-start.2 = (f32[3,17,33,1]{2,3,1,0:T(1,128)S(1)}, f32[3,17,33,1]{2,3,1,0:T(1,128)S(1)}, u32[]{:S(2)}, u32[]{:S(2)}) collective-permute-start(f32[3,17,33,1]{2,3,1,0:T(1,128)S(1)} %copy.11), channel_id=1, source_target_pairs={{1,0},{2,1},{3,2},{4,3},{5,4},{6,5},{7,6},{9,8},{10,9},{11,10},{12... | collective-permute-start | bytes 20204 | tf_op jit(solution)/shard_map/ppermute | solution.py:19
  32.0 1.9 pad_maximum_fusion
  33.9 116.0 %while.10 = (s32[]{:T(128)}, f32[16,32,256]{2,1,0:T(8,128)S(1)}, s32[16]{0:T(128)S(1)}, f32[3,17,33,257]{3,2,1,0:T(8,128)}, f32[24,24]{1,0:T(8,128)S(1)}, /*index=5*/s32[]{:T(128)}, s32[]{:T(128)}, s32[]{}, s32[]{:T(128)}, s32[]{}) while((s32[]{:T(128)}, f32[16,32,256]{2,1,0:T(8,128)S(1)}, s32[16]{0:T(128)S(1)}, f32[3,17,33,257]{3,2,1,0:T(8,128)}, ...), condition=%wide.region_2.3_spmd, body=%wide.region_0.2_spmd.sunk | while | flops 57008136 | bytes 5671371 | solution.py:86
  36.4 1.5 dynamic-slice_bitcast_fusion.25
  43.5 1.5 dynamic-slice_bitcast_fusion.25
  50.7 1.8 dynamic-slice_bitcast_fusion.25
  58.0 1.7 dynamic-slice_bitcast_fusion.25
  65.3 1.6 dynamic-slice_bitcast_fusion.25
  72.6 1.6 dynamic-slice_bitcast_fusion.25
  79.8 1.6 dynamic-slice_bitcast_fusion.25
  87.1 1.6 dynamic-slice_bitcast_fusion.25
  94.3 1.7 dynamic-slice_bitcast_fusion.25
  101.6 1.8 dynamic-slice_bitcast_fusion.25
  109.0 1.6 dynamic-slice_bitcast_fusion.25
  116.2 1.7 dynamic-slice_bitcast_fusion.25
  123.6 1.6 dynamic-slice_bitcast_fusion.25
  130.8 1.6 dynamic-slice_bitcast_fusion.25
  138.0 1.6 dynamic-slice_bitcast_fusion.25
  145.2 1.6 dynamic-slice_bitcast_fusion.25
  153.3 3.7 %collective-permute-done.4 = f32[2,32,256]{2,1,0:T(8,128)S(1)} collective-permute-done((f32[2,32,256]{2,1,0:T(8,128)S(1)}, f32[2,32,256]{2,1,0:T(8,128)S(1)}, u32[]{:S(2)}, u32[]{:S(2)}) %collective-permute-start.4) | collective-permute-done | bytes 65568 | tf_op jit(solution)/shard_map/ppermute | solution.py:30
  159.6 3.4 %collective-permute-done.6 = f32[20,2,256]{2,1,0:T(2,128)S(1)} collective-permute-done((f32[20,2,256]{2,1,0:T(2,128)S(1)}, f32[20,2,256]{2,1,0:T(2,128)S(1)}, u32[]{:S(2)}, u32[]{:S(2)}) %collective-permute-start.6) | collective-permute-done | bytes 40992 | tf_op jit(solution)/shard_map/ppermute | solution.py:30
  163.4 2.4 collective-permute-start.7
  165.7 4.0 %collective-permute-start.8 = (f32[20,36,2]{2,1,0:T(8,128)S(1)}, f32[20,36,2]{2,1,0:T(8,128)S(1)}, u32[]{:S(2)}, u32[]{:S(2)}) collective-permute-start(f32[20,36,2]{2,1,0:T(8,128)S(1)} %get-tuple-element.84), channel_id=1, source_target_pairs={{1,0},{2,1},{3,2},{4,3},{5,4},{6,5},{7,6},{9,8},{10,9},{11,10},{12... | collective-permute-start | bytes 17288 | tf_op jit(solution)/shard_map/ppermute | solution.py:30
  169.7 22.7 %all-reduce.4 = (f32[]{:T(128)}, f32[]{:T(128)}) all-reduce(f32[]{:T(128)} %get-tuple-element.37, f32[]{:T(128)} %get-tuple-element.36), channel_id=1, replica_groups=mesh['gx_0'=2,'gx_1'=8,'gy'=8,'gz_0'=4,'gz_1'=2] {'gx_0'}, use_global_device_ids=true, to_apply=%region_4.5 | all-reduce | flops 2 | bytes 16 | tf_op jit(solution)/shard_map/psum | solution.py:37
  192.4 19.1 %all-reduce.1 = (f32[]{:T(128)}, f32[]{:T(128)}) all-reduce(f32[]{:T(128)} %get-tuple-element.56, f32[]{:T(128)} %get-tuple-element.57), channel_id=1, replica_groups=mesh['gx_0'=2,'gx_1'=8,'gy'=8,'gz_0'=4,'gz_1'=2] {'gx_1'}, use_global_device_ids=true, to_apply=%region_5.6 | all-reduce | flops 2 | bytes 16 | tf_op jit(solution)/shard_map/psum | solution.py:37
  211.5 15.5 %all-reduce = (f32[]{:T(128)}, f32[]{:T(128)}) all-reduce(f32[]{:T(128)} %get-tuple-element.50, f32[]{:T(128)} %get-tuple-element.51), channel_id=1, replica_groups=mesh['gx_0'=2,'gx_1'=8,'gy'=8,'gz_0'=4,'gz_1'=2] {'gy'}, use_global_device_ids=true, to_apply=%region_6.7 | all-reduce | flops 2 | bytes 16 | tf_op jit(solution)/shard_map/psum | solution.py:37
  227.1 8.1 %all-reduce.2 = (f32[]{:T(128)}, f32[]{:T(128)}) all-reduce(f32[]{:T(128)} %get-tuple-element.48, f32[]{:T(128)} %get-tuple-element.49), channel_id=1, replica_groups=mesh['gx_0'=2,'gx_1'=8,'gy'=8,'gz_0'=4,'gz_1'=2] {'gz_0'}, use_global_device_ids=true, to_apply=%region_7.8 | all-reduce | flops 2 | bytes 16 | tf_op jit(solution)/shard_map/psum | solution.py:37
  235.2 14.1 %all-reduce.3 = (f32[]{:T(128)}, f32[]{:T(128)}) all-reduce(f32[]{:T(128)} %get-tuple-element.52, f32[]{:T(128)} %get-tuple-element.53), channel_id=1, replica_groups=mesh['gx_0'=2,'gx_1'=8,'gy'=8,'gz_0'=4,'gz_1'=2] {'gz_1'}, use_global_device_ids=true, to_apply=%region_8.9 | all-reduce | flops 2 | bytes 16 | tf_op jit(solution)/shard_map/psum | solution.py:37
  251.8 1.4 slice_add_fusion.2
  (499 shorter events, 67.9 us)
Async XLA Ops:
  1.5 7.7 %collective-permute-start = (f32[3,1,32,256]{3,2,1,0:T(8,128)S(1)}, f32[3,1,32,256]{3,2,1,0:T(8,128)S(1)}, u32[]{:S(2)}, u32[]{:S(2)}) collective-permute-start(f32[3,1,32,256]{3,2,1,0:T(8,128)S(1)} %slice.144), channel_id=1, source_target_pairs={{64,0},{128,64},{192,128},{256,192},{320,256},{384,320},{448,384},... | collective-permute-start | bytes 294920 | tf_op jit(solution)/shard_map/ppermute | solution.py:19
  9.3 5.3 %collective-permute-start.1 = (f32[3,17,1,256]{3,2,1,0:T(1,128)S(1)}, f32[3,17,1,256]{3,2,1,0:T(1,128)S(1)}, u32[]{:S(2)}, u32[]{:S(2)}) collective-permute-start(f32[3,17,1,256]{3,2,1,0:T(1,128)S(1)} %slice.168), channel_id=1, source_target_pairs={{8,0},{16,8},{24,16},{32,24},{40,32},{48,40},{56,48},{9,1},{17,9},... | collective-permute-start | bytes 156680 | tf_op jit(solution)/shard_map/ppermute | solution.py:19
  15.2 16.3 %collective-permute-start.2 = (f32[3,17,33,1]{2,3,1,0:T(1,128)S(1)}, f32[3,17,33,1]{2,3,1,0:T(1,128)S(1)}, u32[]{:S(2)}, u32[]{:S(2)}) collective-permute-start(f32[3,17,33,1]{2,3,1,0:T(1,128)S(1)} %copy.11), channel_id=1, source_target_pairs={{1,0},{2,1},{3,2},{4,3},{5,4},{6,5},{7,6},{9,8},{10,9},{11,10},{12... | collective-permute-start | bytes 20204 | tf_op jit(solution)/shard_map/ppermute | solution.py:19
  32.0 1.9 copy-start.1
  33.9 116.0 %copy-start = (f32[16,32,256]{2,1,0:T(8,128)S(1)}, f32[16,32,256]{2,1,0:T(8,128)}, u32[]{:S(2)}) copy-start(f32[16,32,256]{2,1,0:T(8,128)} %param.6) | copy-start | bytes 1572868
  150.7 2.6 %collective-permute-start.3 = (f32[2,32,256]{2,1,0:T(8,128)S(1)}, f32[2,32,256]{2,1,0:T(8,128)S(1)}, u32[]{:S(2)}, u32[]{:S(2)}) collective-permute-start(f32[2,32,256]{2,1,0:T(8,128)S(1)} %get-tuple-element.87), channel_id=1, source_target_pairs={{0,64},{64,128},{128,192},{192,256},{256,320},{320,384},{384,448},... | collective-permute-start | bytes 196616 | tf_op jit(solution)/shard_map/ppermute | solution.py:29
  152.0 5.0 %collective-permute-start.4 = (f32[2,32,256]{2,1,0:T(8,128)S(1)}, f32[2,32,256]{2,1,0:T(8,128)S(1)}, u32[]{:S(2)}, u32[]{:S(2)}) collective-permute-start(f32[2,32,256]{2,1,0:T(8,128)S(1)} %get-tuple-element.88), channel_id=1, source_target_pairs={{64,0},{128,64},{192,128},{256,192},{320,256},{384,320},{448,384},... | collective-permute-start | bytes 196616 | tf_op jit(solution)/shard_map/ppermute | solution.py:30
  157.0 2.6 %collective-permute-start.5 = (f32[20,2,256]{2,1,0:T(2,128)S(1)}, f32[20,2,256]{2,1,0:T(2,128)S(1)}, u32[]{:S(2)}, u32[]{:S(2)}) collective-permute-start(f32[20,2,256]{2,1,0:T(2,128)S(1)} %get-tuple-element.85), channel_id=1, source_target_pairs={{0,8},{8,16},{16,24},{24,32},{32,40},{40,48},{48,56},{1,9},{9,17},... | collective-permute-start | bytes 122888 | tf_op jit(solution)/shard_map/ppermute | solution.py:29
  158.3 4.7 %collective-permute-start.6 = (f32[20,2,256]{2,1,0:T(2,128)S(1)}, f32[20,2,256]{2,1,0:T(2,128)S(1)}, u32[]{:S(2)}, u32[]{:S(2)}) collective-permute-start(f32[20,2,256]{2,1,0:T(2,128)S(1)} %get-tuple-element.86), channel_id=1, source_target_pairs={{8,0},{16,8},{24,16},{32,24},{40,32},{48,40},{56,48},{9,1},{17,9},... | collective-permute-start | bytes 122888 | tf_op jit(solution)/shard_map/ppermute | solution.py:30
  163.4 87.2 %collective-permute-start.7 = (f32[20,36,2]{2,1,0:T(8,128)S(1)}, f32[20,36,2]{2,1,0:T(8,128)S(1)}, u32[]{:S(2)}, u32[]{:S(2)}) collective-permute-start(f32[20,36,2]{2,1,0:T(8,128)S(1)} %get-tuple-element.83), channel_id=1, source_target_pairs={{0,1},{1,2},{2,3},{3,4},{4,5},{5,6},{6,7},{8,9},{9,10},{10,11},{11... | collective-permute-start | bytes 17288 | tf_op jit(solution)/shard_map/ppermute | solution.py:29
  165.7 84.9 %collective-permute-start.8 = (f32[20,36,2]{2,1,0:T(8,128)S(1)}, f32[20,36,2]{2,1,0:T(8,128)S(1)}, u32[]{:S(2)}, u32[]{:S(2)}) collective-permute-start(f32[20,36,2]{2,1,0:T(8,128)S(1)} %get-tuple-element.84), channel_id=1, source_target_pairs={{1,0},{2,1},{3,2},{4,3},{5,4},{6,5},{7,6},{9,8},{10,9},{11,10},{12... | collective-permute-start | bytes 17288 | tf_op jit(solution)/shard_map/ppermute | solution.py:30
where the time goes:
time: 258 us; the launch traced here: 256 us
  blocking collectives  79.5 us (31%)
  local copies, waits for them, and re-layouts  71.4 us (28%)
  loops' own time  35 us (14%)
  starting transfers between devices  29.6 us (11%)
  waiting for transfers between devices  16.8 us (7%)
  matrix products  13.2 us (5%)
  other arithmetic  5.65 us (2%)
  between operations  4.41 us (2%)
    psum x5, blocking collectives, over_axes(): shard = lax.psum(shard, axis)  79.5 us
    while x400, local copies, waits for them, and re-layouts  39.6 us
    another operation x1, loops' own time, energies(): return lax.map(one_plane, jnp.arange(planes, dtype=jnp.int32))  35 us
    another operation x16, local copies, waits for them, and re-layouts, plane_energy(): jnp.stack([slab_nodes[member, along_x, along_y:along_y + height, along_z:...  18.5 us
    ppermute x3, starting transfers between devices, from_behind(): return lax.ppermute(block, axis, route)  18.1 us
    dot_general x16, matrix products, plane_energy(): jnp.dot(stiffness, corner_rows, precision=lax.Precision.HIGHEST, preferre...  13.2 us
    ppermute x3, waiting for transfers between devices, from_behind(): return lax.ppermute(block, axis, route)  9.6 us
    dynamic_slice x16, local copies, waits for them, and re-layouts, energies(): return lax.map(one_plane, jnp.arange(planes, dtype=jnp.int32))  9.38 us
  transfers between devices with their start and end apart: 9, of which 5 were waited for; matrix products, arithmetic and copies ran while one was open for 1% of the time, Pallas kernels for 0%

commit v1 on v0

v1 whole, which is shorter than its diff:
```python
import functools

import jax
import jax.numpy as jnp
from jax import lax
from jax.experimental import pallas as pl
from jax.experimental.pallas import tpu as pltpu
from jax.sharding import PartitionSpec as P

VOID = 0.001
MESH = pl.DeviceIdType.MESH
F32 = jnp.float32

S_Y, S_Z, S_YZ, S_XM, S_XY, S_XZ, S_RM, S_RY, S_RZ = range(9)
S_ZL, S_ZR, S_YD, S_YU, S_XD, S_XU, S_RF = range(9, 16)
S_XYZ, S_RYZ = 16, 17
N_SEM = 18
GO_U, GO_R = 3, 4
UNROLL_PREP, UNROLL_MAIN, UNROLL_LAST = 4, 7, 5


def rounded(v):
    return v.astype(jnp.bfloat16).astype(F32)


def taps_sum(position, extent):
    low = jnp.minimum(position, extent - 1 - position)
    return jnp.where(low == 0, F32(1 / 6), jnp.where(low == 1, F32(1 / 8), F32(1 / 9)))


def kernel(nx, ny, px, py, pz,
           disp, dens, stiff,
           out, sums,
           U, UH, G, HR, R, W, Z, F, T, L, KV, INV,
           YS, YH, HY, GY, ZS, ZX, RU, RY, RZ,
           CL, CR, CLr, CRr, YS2, YR, RF, A1, A2, A3,
           load_sem, send_sem, recv_sem, ar_send, ar_recv, go):
    gx, gy, gz = lax.axis_index("gx"), lax.axis_index("gy"), lax.axis_index("gz")
    half = px // 2
    xh, zc = gx // half, gx % half
    lane32 = lax.broadcasted_iota(jnp.int32, (32, 128), 1)
    nq = 3 * nx
    npz = 2 * pz

    def dev(x, y, z):
        return {"gx": x, "gy": y, "gz": z}

    def remote(src, dst, slot, x, y, z):
        return pltpu.make_async_remote_copy(
            src_ref=src, dst_ref=dst, send_sem=send_sem.at[slot], recv_sem=recv_sem.at[slot],
            device_id=dev(x, y, z), device_id_type=MESH)

    def when(cond, *actions):
        @pl.when(cond)
        def _():
            for act in actions:
                act()

    def wait(name, *pairs):
        with jax.named_scope(name):
            for cond, *actions in pairs:
                when(cond, *actions)

    has_yl, has_yu = gy > 0, gy < py - 1
    has_zl, has_zu = gz > 0, gz < pz - 1
    last_x, first_x, upper0, lower1 = gx == px - 1, gx == 0, gx == half, gx == half - 1
    not_last, not_first = gx < px - 1, gx > 0
    plain_down = not_first & (gx != half)

    bar = pltpu.get_barrier_semaphore()

    def signal(x, y, z):
        pl.semaphore_signal(bar, inc=1, device_id=dev(x, y, z), device_id_type=MESH)

    def signal_go(slot, x, y, z):
        pl.semaphore_signal(go.at[slot], inc=1, device_id=dev(x, y, z), device_id_type=MESH)

    def as_int(c):
        return c.astype(jnp.int32)

    key_x = xh * pz + gz
    hy = py // 2
    key_y = jnp.where(gy < hy, gy, py - 1 + hy - gy)
    key_z = zc

    def of_x(k):
        return (k // pz) * half + zc, gy, k % pz

    def of_y(k):
        return gx, jnp.where(k < hy, k, py - 1 + hy - k), gz

    def of_z(k):
        return xh * half + k, gy, gz

    groups = ((key_x, npz, of_x), (key_y, py, of_y), (key_z, half, of_z))

    when(has_zu, lambda: signal(gx, gy, gz + 1))
    when(has_zl, lambda: signal(gx, gy, gz - 1))
    when(has_yu, lambda: signal(gx, gy + 1, gz))
    when(has_yl, lambda: signal(gx, gy - 1, gz))
    when(has_yu & has_zu, lambda: signal(gx, gy + 1, gz + 1))
    when(upper0, lambda: signal(half - 1, gy, gz))

    def edges(x, cond):
        when(cond & has_yu, lambda: signal(x, gy + 1, gz))
        when(cond & has_zu, lambda: signal(x, gy, gz + 1))
        when(cond & has_yu & has_zu, lambda: signal(x, gy + 1, gz + 1))

    edges(gx + 1, not_last & (gx != half - 1))
    edges(half, first_x)
    for key, count, where_to in groups:
        def tell(k, c, where_to=where_to):
            signal(*where_to(k))
            return c

        lax.fori_loop(key + 1, count, tell, 0)
    n_wait = as_int(has_zu) + as_int(has_zl) + as_int(has_yu) + as_int(has_yl) + as_int(has_yl & has_zl) + as_int(lower1)
    n_wait = n_wait + key_x + key_y + key_z
    n_wait = n_wait + jnp.where(first_x, 0, as_int(has_yl) + as_int(has_zl) + as_int(has_yl & has_zl))

    loads = []
    for t in range(2):
        for m in range(3):
            loads.append(pltpu.make_async_copy(
                disp.at[m, :, :, pl.ds(128 * t, 128)], U.at[pl.ds(0, nx), m, t], load_sem.at[3 * t + m]))
    loads.append(pltpu.make_async_copy(stiff, KV, load_sem.at[8]))
    for t in range(2):
        loads.append(pltpu.make_async_copy(dens.at[:, :, pl.ds(128 * t, 128)], R.at[:, t], load_sem.at[6 + t]))
    for c in loads:
        c.start()

    with jax.named_scope("w_bar"):
        pl.semaphore_wait(bar, n_wait)
    when(lower1, lambda: signal_go(GO_R, 0, gy, gz))

    zero8 = jnp.zeros((8, 128), F32)
    zero32 = jnp.zeros((32, 128), F32)

    @pl.when(last_x)
    def _():
        for m in range(3):
            for t in range(2):
                U[nx, m, t] = zero32
        for t in range(2):
            YH[t, nq:nq + 8, :] = zero8
            F[nx + 2, t] = zero32
            F[nx + 3, t] = zero32
        ZX[1] = jnp.zeros((40, 128), F32)

    @pl.when(first_x)
    def _():
        for t in range(2):
            F[0, t] = zero32
            F[1, t] = zero32

    @pl.when(gy == py - 1)
    def _():
        for t in range(2):
            YH[t] = jnp.zeros((nq + 8, 128), F32)
            YR[1, t] = jnp.zeros((2 * nx, 128), F32)

    @pl.when(gy == 0)
    def _():
        for t in range(2):
            YR[0, t] = jnp.zeros((2 * nx, 128), F32)

    @pl.when(gz == pz - 1)
    def _():
        ZX[0, 0:32, :] = zero32
        ZX[1, 0:32, :] = zero32
        CLr[...] = zero32

    @pl.when((gz == pz - 1) | (gy == py - 1))
    def _():
        ZX[0, 32:40, :] = zero8
        ZX[1, 32:40, :] = zero8

    @pl.when(gz == 0)
    def _():
        CRr[...] = zero32

    for t in range(2):
        zr = lax.broadcasted_iota(jnp.int32, (256, 128), 0)
        zl = lax.broadcasted_iota(jnp.int32, (256, 128), 1) + 128 * t
        T[:, 128 * t:128 * t + 128] = jnp.maximum(3 - jnp.abs(zr - zl), 0).astype(F32).astype(jnp.bfloat16)
        yv = lax.broadcasted_iota(jnp.int32, (32, 128), 0) + gy * ny
        zv = lane32 + 128 * t + gz * 256
        INV[t] = (F32(-3.0 * (1.0 - VOID)) * taps_sum(yv, py * ny)) * taps_sum(zv, pz * 256)
    HR[...] = jnp.zeros(HR.shape, F32)

    with jax.named_scope("w_load0"):
        for c in loads[:3]:
            c.wait()
    Uf = U.reshape((nx + 1) * 3 * 2 * 32, 128)
    with jax.named_scope("c_packz"):
        acc = zero32
        for q in range(nq):
            acc = jnp.where(lane32 == q, jnp.broadcast_to(U[q // 3, q % 3, 0, :, 0:1], (32, 128)), acc)
        ZS[...] = acc
        YS[0] = Uf[pl.ds(0, nq, stride=64), :]
    with jax.named_scope("w_load1"):
        for c in loads[3:6]:
            c.wait()
    YS[1] = Uf[pl.ds(32, nq, stride=64), :]

    y_copy = remote(YS, YH.at[:, pl.ds(0, nq), :], S_Y, gx, gy - 1, gz)
    z_copy = remote(ZS, ZX.at[0, pl.ds(0, 32), :], S_Z, gx, gy, gz - 1)
    yz_copy = remote(ZS.at[pl.ds(0, 8), :], ZX.at[0, pl.ds(32, 8), :], S_YZ, gx, gy - 1, gz - 1)
    xm_copy = remote(U.at[0], U.at[nx], S_XM, gx - 1, gy, gz)
    xm_to_relay = remote(U.at[0], RU, S_RM, 0, gy, gz)
    xm_relay = remote(RU, U.at[nx], S_XM, half - 1, gy, gz)
    xy_copy = remote(YS.at[:, pl.ds(0, 8), :], YH.at[:, pl.ds(nq, 8), :], S_XY, gx - 1, gy - 1, gz)
    xy_to_relay = remote(YS.at[:, pl.ds(0, 8), :], RY, S_RY, 0, gy - 1, gz)
    xy_relay = remote(RY, YH.at[:, pl.ds(nq, 8), :], S_XY, half - 1, gy, gz)
    xz_copy = remote(ZS, ZX.at[1, pl.ds(0, 32), :], S_XZ, gx - 1, gy, gz - 1)
    xz_to_relay = remote(ZS, RZ.at[pl.ds(0, 32), :], S_RZ, 0, gy, gz - 1)
    xz_relay = remote(RZ.at[pl.ds(0, 32), :], ZX.at[1, pl.ds(0, 32), :], S_XZ, half - 1, gy, gz)
    xyz_copy = remote(ZS.at[pl.ds(0, 8), :], ZX.at[1, pl.ds(32, 8), :], S_XYZ, gx - 1, gy - 1, gz - 1)
    xyz_to_relay = remote(ZS.at[pl.ds(0, 8), :], RZ.at[pl.ds(32, 8), :], S_RYZ, 0, gy - 1, gz - 1)
    xyz_relay = remote(RZ.at[pl.ds(32, 8), :], ZX.at[1, pl.ds(32, 8), :], S_XYZ, half - 1, gy, gz)
    both_l, both_u = has_yl & has_zl, has_yu & has_zu

    when(has_zl, z_copy.start)
    when(has_yl & has_zl, yz_copy.start)
    when(has_yl, y_copy.start)
    when(plain_down, xm_copy.start)
    when(upper0, xm_to_relay.start)
    when(plain_down & has_yl, xy_copy.start)
    when(plain_down & has_zl, xz_copy.start)
    when(plain_down & both_l, xyz_copy.start)
    when(upper0 & has_yl, xy_to_relay.start)
    when(upper0 & has_zl, xz_to_relay.start)
    when(upper0 & both_l, xyz_to_relay.start)

    loads[6].wait()
    kv = KV[...]
    k_hi = rounded(kv)
    k_lo = kv - k_hi
    dr = lax.broadcasted_iota(jnp.int32, (24, 256), 0)
    cc = lax.broadcasted_iota(jnp.int32, (24, 256), 1)
    second = cc >= 112
    cl = jnp.where(second, cc - 112, cc)
    inside = cc < 224
    tau = cl >> 3
    in_main = cl < 96
    a_m = as_int(tau >= 6)
    a_ = jnp.where(in_main, a_m, (cl - 96) >> 3)
    mc_ = jnp.where(in_main, tau - 6 * a_m, cl & 7)
    ok = inside & (mc_ < 6)
    d0 = 8 * (mc_ >> 1) + 4 * a_ + (mc_ & 1)
    kb = []
    for b in range(2):
        pick = ok & (dr == d0 + 2 * b)
        b_hi = jnp.where(pick & jnp.logical_not(second), F32(1), F32(0))
        b_lo = jnp.where(pick & second, F32(1), F32(0))
        kb.append(jnp.dot(k_hi, b_hi, preferred_element_type=F32) + jnp.dot(k_lo, b_lo, preferred_element_type=F32))
    cy = lax.broadcasted_iota(jnp.int32, (16, 256), 1)
    yy = lax.broadcasted_iota(jnp.int32, (16, 256), 0) & 7
    cy = jnp.where(cy >= 112, cy - 112, cy)
    rr = jnp.where(cy < 96, cy & 7, 8)
    m0, m1 = rr == yy, rr == yy + 1
    for d in range(0, 24, 2):
        r0, r1 = (jnp.concatenate([jnp.broadcast_to(kb[b][d + k:d + k + 1, :], (8, 256)) for k in range(2)], axis=0)
                  for b in range(2))
        L[8 * d:8 * d + 16, :] = jnp.where(m0, r0, jnp.where(m1, r1, F32(0))).astype(jnp.bfloat16)

    def store_pair(p, m, t, x0, x1):
        for j in range(4):
            x = jnp.concatenate([x0[8 * j:8 * j + 8], x1[8 * j:8 * j + 8]], axis=0)
            h = x.astype(jnp.bfloat16)
            UH[p, m, t, j] = h
            g = 2.0 * x - h.astype(F32)
            G[0, p, m, t, 8 * j:8 * j + 8, :] = g[0:8]
            G[1, p, m, t, 8 * j:8 * j + 8, :] = g[8:16]
            if j > 0:
                HR[p, t, 8 * j - 8 + 2 * m:8 * j - 7 + 2 * m, :] = x0[8 * j:8 * j + 1]
                HR[p, t, 8 * j - 7 + 2 * m:8 * j - 6 + 2 * m, :] = x1[8 * j:8 * j + 1]

    def prep(p, m, zx):
        u0, u1 = U[p, m, 0], U[p, m, 1]
        s0, s1 = pltpu.roll(u0, 127, 1), pltpu.roll(u1, 127, 1)
        store_pair(p, m, 0, u0, jnp.where(lane32 == 127, s1, s0))
        store_pair(p, m, 1, u1, jnp.where(lane32 == 127, zx, s1))

    for slot, (key, count, where_to) in enumerate(groups):
        def tell(k, c, slot=slot, where_to=where_to):
            signal_go(slot, *where_to(k))
            return c

        lax.fori_loop(0, key, tell, 0)
    when(zc > 0, lambda: signal_go(GO_U, gx - 1, gy, gz))

    wait("w_z", (has_zu, z_copy.wait_recv))
    with jax.named_scope("c_prep"):
        def prep_planes(p, carry):
            for m in range(3):
                prep(p, m, pltpu.roll(ZX[0, 0:32, :], 127 - (3 * p + m), 1))
            return carry

        lax.fori_loop(0, nx, prep_planes, 0, unroll=UNROLL_PREP)

    Gf = G.reshape(2 * (nx + 1) * 3 * 2 * 40, 128)
    HRf = HR.reshape((nx + 1) * 2 * 32, 128)

    def halo_rows(first, count, zx_row, planes):
        lanes = lax.broadcasted_iota(jnp.int32, (count, 128), 1)
        rows = lax.broadcasted_iota(jnp.int32, (count, 128), 0)
        nxt = jnp.sum(jnp.where(lanes == rows, jnp.broadcast_to(zx_row, (count, 128)), 0.0), axis=1, keepdims=True)
        u0, u1 = YH[0, first:first + count, :], YH[1, first:first + count, :]
        s0, s1 = pltpu.roll(u0, 127, 1), pltpu.roll(u1, 127, 1)
        v0 = jnp.where(lanes == 127, s1, s0)
        v1 = jnp.where(lanes == 127, jnp.broadcast_to(nxt, (count, 128)), s1)
        for c, pair in enumerate(((u0, u1), (v0, v1))):
            for t in range(2):
                HY[c, t, first:first + count, :] = pair[t]
                GY[c, t, first:first + count, :] = 2.0 * pair[t] - rounded(pair[t])
        for c in range(2):
            for t in range(2):
                n = 3 * planes
                at = ((c * (nx + 1) + first // 3) * 6 + t) * 40 + 32
                Gf[pl.ds(at, n, stride=80), :] = GY[c, t, first:first + n, :]
                for m in range(3):
                    at = ((first // 3) * 2 + t) * 32 + 24 + 2 * m + c
                    if planes == 1:
                        HRf[at:at + 1, :] = HY[c, t, first + m:first + m + 1, :]
                    else:
                        HRf[pl.ds(at, planes, stride=64), :] = HY[c, t, pl.ds(first + m, planes, stride=3), :]

    def blocks(i, js, acc):
        comp, vol = acc
        rx = taps_sum(gx * nx + i, px * nx)
        for j in js:
            r0 = 8 * j
            cols = []
            for t in range(2):
                tiles = [UH[i + a, m, t, j] for a in range(2) for m in range(3)]
                tiles.append(jnp.concatenate([HR[i, t, r0:r0 + 8, :], HR[i + 1, t, r0:r0 + 8, :]], axis=0).astype(jnp.bfloat16))
                cols.append(jnp.concatenate(tiles, axis=0))
            rhs = jnp.concatenate(cols, axis=1)
            rhs = jnp.concatenate([rhs, rhs], axis=0)
            prod = jnp.dot(L[:, 0:224], rhs, preferred_element_type=F32)
            for t in range(2):
                e = None
                for d in range(24):
                    m, a, b, c = d // 8, (d // 4) % 2, (d // 2) % 2, d % 2
                    term = prod[8 * d:8 * d + 8, 128 * t:128 * t + 128] * G[c, i + a, m, t, pl.ds(r0 + b, 8), :]
                    e = term if e is None else e + term
                rho = R[i, t, r0:r0 + 8, :]
                r2 = rho * rho
                comp = comp + (VOID + (r2 * rho) * (1.0 - VOID)) * e
                vol = vol + rho
                W[i, t, r0:r0 + 8, :] = (r2 * e) * (INV[t, r0:r0 + 8, :] * rx)
        return comp, vol

    for c in loads[7:9]:
        c.wait()
    first_part = (nx - 1) // 2
    with jax.named_scope("c_main0"):
        acc = lax.fori_loop(0, first_part, lambda i, a: blocks(i, (0, 1, 2), a), (zero8, zero8), unroll=UNROLL_MAIN)
    with jax.named_scope("c_main1"):
        acc = lax.fori_loop(first_part, nx - 1, lambda i, a: blocks(i, (0, 1, 2), a), acc, unroll=UNROLL_MAIN)
    wait("w_yz", (both_u, yz_copy.wait_recv))
    wait("w_y", (has_yu, y_copy.wait_recv))
    with jax.named_scope("c_halo"):
        halo_rows(0, nq, ZX[0, 32:33, :], nx)
    with jax.named_scope("c_main2"):
        acc = lax.fori_loop(0, nx - 1, lambda i, a: blocks(i, (3,), a), acc, unroll=UNROLL_LAST)

    def relay():
        pl.semaphore_wait(go.at[GO_R], 1)
        xm_to_relay.wait_recv()
        xm_relay.start()
        when(has_yu, xy_to_relay.wait_recv, xy_relay.start)
        when(has_zu, xz_to_relay.wait_recv, xz_relay.start)
        when(both_u, xyz_to_relay.wait_recv, xyz_relay.start)

    wait("w_xm", (not_last, xm_copy.wait_recv))
    wait("w_xe", (not_last & has_yu, xy_copy.wait_recv), (not_last & has_zu, xz_copy.wait_recv),
         (not_last & both_u, xyz_copy.wait_recv))
    with jax.named_scope("c_last"):
        for m in range(3):
            prep(nx, m, pltpu.roll(ZX[1, 0:32, :], 127 - m, 1))
        halo_rows(nq, 8, ZX[1, 32:33, :], 1)
        comp, vol = blocks(nx - 1, (0, 1, 2, 3), acc)

    def stage_send(buf, stage):
        key, count, where_to = groups[stage]
        with jax.named_scope(f"w_go{stage}"):
            when(key < count - 1, lambda: pl.semaphore_wait(go.at[stage], count - 1 - key))

        def send(k, c):
            pltpu.make_async_remote_copy(
                src_ref=buf.at[key], dst_ref=buf.at[key], send_sem=ar_send.at[stage], recv_sem=ar_recv.at[stage],
                device_id=dev(*where_to(k)), device_id_type=MESH).start()
            return c

        lax.fori_loop(0, key, send, 0)
        lax.fori_loop(key + 1, count, send, 0)

    def stage_wait(buf, stage):
        count = groups[stage][1]
        part = buf.at[pl.ds(0, count - 1)]
        with jax.named_scope(f"w_ar{stage}"):
            pltpu.make_async_copy(part, part, ar_recv.at[stage]).wait()
        total = buf[0]
        for k in range(1, count):
            total = total + buf[k]
        return total

    def stage_done(buf, stage):
        part = buf.at[pl.ds(0, groups[stage][1] - 1)]
        pltpu.make_async_copy(part, part, ar_send.at[stage]).wait()

    lane1 = lax.broadcasted_iota(jnp.int32, (1, 128), 1)
    comp_all = jnp.sum(jnp.sum(comp, axis=0, keepdims=True), axis=1, keepdims=True)
    vol_all = jnp.sum(jnp.sum(vol, axis=0, keepdims=True), axis=1, keepdims=True)
    A1[key_x] = jnp.where(lane1 == 0, jnp.broadcast_to(comp_all, (1, 128)), jnp.broadcast_to(vol_all, (1, 128)))
    stage_send(A1, 0)

    with jax.named_scope("c_packw"):
        lo, hi = zero32, zero32
        for p in range(nx):
            w0, w1 = W[p, 0], W[p, 1]
            for k in range(2):
                lo = jnp.where(lane32 == 2 * p + k, jnp.broadcast_to(w0[:, k:k + 1], (32, 128)), lo)
                hi = jnp.where(lane32 == 2 * p + k, jnp.broadcast_to(w1[:, 126 + k:127 + k], (32, 128)), hi)
        even = (lane32 & 1) == 0
        CL[...] = jnp.where(even, lo, lo + 2.0 * pltpu.roll(lo, 1, 1))
        CR[...] = jnp.where(even, hi + 2.0 * pltpu.roll(hi, 127, 1), hi)
    zl_copy = remote(CL, CLr, S_ZL, gx, gy, gz - 1)
    zr_copy = remote(CR, CRr, S_ZR, gx, gy, gz + 1)
    when(has_zl, zl_copy.start)
    when(has_zu, zr_copy.start)

    def filter_z(g, carry):
        w = jnp.concatenate([jnp.concatenate([W[4 * g + k, 0], W[4 * g + k, 1]], axis=1) for k in range(4)], axis=0)
        w_hi = w.astype(jnp.bfloat16)
        w_lo = (w - w_hi.astype(F32)).astype(jnp.bfloat16)
        z = jnp.dot(w_hi, T[...], preferred_element_type=F32) + jnp.dot(w_lo, T[...], preferred_element_type=F32)
        for k in range(4):
            for t in range(2):
                Z[4 * g + k, t, 8:40, :] = z[32 * k:32 * k + 32, 128 * t:128 * t + 128]
        return carry

    with jax.named_scope("c_fz"):
        lax.fori_loop(0, nx // 4, filter_z, 0, unroll=True)

    wait("w_relay", (first_x, relay))
    wait("w_wz", (has_zu, zl_copy.wait_recv), (has_zl, zr_copy.wait_recv))
    with jax.named_scope("c_fixz"):
        left, right = CRr[...], CLr[...]
        for p in range(nx):
            Z[p, 0, 8:40, :] += jnp.where(lane32 < 2, pltpu.roll(left, (128 - 2 * p) % 128, 1), 0.0)
            Z[p, 1, 8:40, :] += jnp.where(lane32 >= 126, pltpu.roll(right, 126 - 2 * p, 1), 0.0)

    Zf = Z.reshape(nx * 2 * 48, 128)
    for t in range(2):
        for r in range(2):
            YS2[0, t, r * nx:(r + 1) * nx, :] = Zf[pl.ds(48 * t + 8 + r, nx, stride=96), :]
            YS2[1, t, r * nx:(r + 1) * nx, :] = Zf[pl.ds(48 * t + 38 + r, nx, stride=96), :]
    yd_copy = remote(YS2.at[0], YR.at[1], S_YD, gx, gy - 1, gz)
    yu_copy = remote(YS2.at[1], YR.at[0], S_YU, gx, gy + 1, gz)
    when(has_yl, yd_copy.start)
    when(has_yu, yu_copy.start)

    total = stage_wait(A1, 0)
    A2[key_y] = total
    stage_send(A2, 1)

    wait("w_wy", (has_yu, yd_copy.wait_recv), (has_yl, yu_copy.wait_recv))
    for t in range(2):
        for r in range(2):
            Zf[pl.ds(48 * t + 6 + r, nx, stride=96), :] = YR[0, t, r * nx:(r + 1) * nx, :]
            Zf[pl.ds(48 * t + 40 + r, nx, stride=96), :] = YR[1, t, r * nx:(r + 1) * nx, :]

    def filter_y(p, carry):
        for t in range(2):
            z = [Z[p, t, 6 + d:38 + d, :] for d in range(5)]
            F[p + 2, t] = 3.0 * z[2] + 2.0 * (z[1] + z[3]) + (z[0] + z[4])
        return carry

    with jax.named_scope("c_fy"):
        lax.fori_loop(0, nx, filter_y, 0, unroll=2)

    xd_copy = remote(F.at[pl.ds(2, 2)], F.at[pl.ds(nx + 2, 2)], S_XD, gx - 1, gy, gz)
    xd_to_relay = remote(F.at[pl.ds(2, 2)], RF, S_RF, 0, gy, gz)
    xd_relay = remote(RF, F.at[pl.ds(nx + 2, 2)], S_XD, half - 1, gy, gz)
    xu_copy = remote(F.at[pl.ds(nx, 2)], F.at[pl.ds(0, 2)], S_XU, gx + 1, gy, gz)
    when(plain_down, xd_copy.start)
    when(upper0, xd_to_relay.start)
    when(zc < half - 1, lambda: pl.semaphore_wait(go.at[GO_U], 1))
    when(not_last, xu_copy.start)

    def filter_x(p, carry):
        for t in range(2):
            f = [F[p + d, t] for d in range(5)]
            out[p, :, 128 * t:128 * t + 128] = 3.0 * f[2] + 2.0 * (f[1] + f[3]) + (f[0] + f[4])
        return carry

    wait("w_frelay", (first_x, xd_to_relay.wait_recv, xd_relay.start))
    with jax.named_scope("c_fx"):
        lax.fori_loop(2, nx - 2, filter_x, 0, unroll=2)
    total = stage_wait(A2, 1)
    A3[key_z] = total
    stage_send(A3, 2)

    wait("w_fd", (not_last, xd_copy.wait_recv))
    for p in (nx - 2, nx - 1):
        filter_x(p, 0)
    wait("w_fu", (not_first, xu_copy.wait_recv))
    for p in (0, 1):
        filter_x(p, 0)

    with jax.named_scope("w_sends"):
        when(has_yl, y_copy.wait_send, yd_copy.wait_send)
        when(has_zl, z_copy.wait_send, zl_copy.wait_send)
        when(has_yl & has_zl, yz_copy.wait_send)
        when(has_zu, zr_copy.wait_send)
        when(has_yu, yu_copy.wait_send)
        when(plain_down, xm_copy.wait_send, xd_copy.wait_send)
        when(plain_down & has_yl, xy_copy.wait_send)
        when(plain_down & has_zl, xz_copy.wait_send)
        when(plain_down & both_l, xyz_copy.wait_send)
        when(upper0, xm_to_relay.wait_send, xd_to_relay.wait_send)
        when(upper0 & has_yl, xy_to_relay.wait_send)
        when(upper0 & has_zl, xz_to_relay.wait_send)
        when(upper0 & both_l, xyz_to_relay.wait_send)
        when(first_x, xm_relay.wait_send, xd_relay.wait_send)
        when(first_x & has_yu, xy_relay.wait_send)
        when(first_x & has_zu, xz_relay.wait_send)
        when(first_x & both_u, xyz_relay.wait_send)
        when(not_last, xu_copy.wait_send)
        stage_done(A1, 0)
        stage_done(A2, 1)
        stage_done(A3, 2)

    total = stage_wait(A3, 2)
    count = F32(px * nx) * F32(py * ny) * F32(pz * 256)
    sums[...] = jnp.broadcast_to(total / count, (8, 128))


def on_device(displacement, density, stiffness):
    px, py, pz = lax.axis_size("gx"), lax.axis_size("gy"), lax.axis_size("gz")
    nx, ny, nz = density.shape
    nq = 3 * nx
    vm = lambda *shape: pltpu.VMEM(shape, F32)
    out, sums = pl.pallas_call(
        functools.partial(kernel, nx, ny, px, py, pz),
        out_shape=(jax.ShapeDtypeStruct((nx, ny, nz), F32), jax.ShapeDtypeStruct((8, 128), F32)),
        in_specs=[pl.BlockSpec(memory_space=pltpu.HBM)] * 3,
        out_specs=(pl.BlockSpec(memory_space=pltpu.VMEM), pl.BlockSpec(memory_space=pltpu.VMEM)),
        scratch_shapes=[
            vm(nx + 1, 3, 2, 32, 128),
            pltpu.VMEM((nx + 1, 3, 2, 4, 16, 128), jnp.bfloat16),
            vm(2, nx + 1, 3, 2, 40, 128),
            vm(nx + 1, 2, 32, 128),
            vm(nx, 2, 32, 128),
            vm(nx, 2, 32, 128),
            vm(nx, 2, 48, 128),
            vm(nx + 4, 2, 32, 128),
            pltpu.VMEM((256, 256), jnp.bfloat16),
            pltpu.VMEM((192, 256), jnp.bfloat16),
            vm(24, 24),
            vm(2, 32, 128),
            vm(2, nq, 128),
            vm(2, nq + 8, 128),
            vm(2, 2, nq + 8, 128),
            vm(2, 2, nq + 8, 128),
            vm(32, 128),
            vm(2, 40, 128),
            vm(3, 2, 32, 128),
            vm(2, 8, 128),
            vm(40, 128),
            vm(32, 128), vm(32, 128), vm(32, 128), vm(32, 128),
            vm(2, 2, 2 * nx, 128),
            vm(2, 2, 2 * nx, 128),
            vm(2, 2, 32, 128),
            vm(2 * pz, 1, 128), vm(py, 1, 128), vm(px // 2, 1, 128),
            pltpu.SemaphoreType.DMA((9,)),
            pltpu.SemaphoreType.DMA((N_SEM,)),
            pltpu.SemaphoreType.DMA((N_SEM,)),
            pltpu.SemaphoreType.DMA((3,)),
            pltpu.SemaphoreType.DMA((3,)),
            pltpu.SemaphoreType.REGULAR((5,)),
        ],
        compiler_params=pltpu.CompilerParams(collective_id=0, has_side_effects=True, vmem_limit_bytes=56_000_000),
    )(displacement, density, stiffness)
    return out, sums[0, 0], sums[0, 1]


def solution(mesh):
    return jax.shard_map(
        on_device,
        mesh=mesh,
        in_specs=(P(None, "gx", "gy", "gz"), P("gx", "gy", "gz"), P()),
        out_specs=(P("gx", "gy", "gz"), P(), P()),
        check_vma=False,
    )
```

time: 258 us -> 43.4 us (0.17)
  the two profiles are of different devices: /device:TPU:1 before, /device:TPU:4 now
where the time goes in v1:
time: 43.4 us; the launch traced here: 43.2 us
  Pallas kernels  40.5 us (93%)
  local copies, waits for them, and re-layouts  2.08 us (5%)
  between operations  0.65 us (1%)
    pallas_call x1, Pallas kernels, on_device(): pl.pallas_call(functools.partial(kernel, nx, ny, px, py, pz), out_shape=(...  40.5 us
    unnamed x3, local copies, waits for them, and re-layouts  1.49 us

profile of v1, /device:TPU:4, one launch (start us, length us, event | category | flops | bytes accessed | tf_op | source)
XLA Modules:
  0.0 43.2 jit_solution(13633127428588921723)
XLA Ops:
  0.6 0.0 copy-start
  0.6 0.7 %copy-done = f32[24,24]{1,0:T(8,128)S(1)} copy-done((f32[24,24]{1,0:T(8,128)S(1)}, f32[24,24]{1,0:T(8,128)}, u32[]{:S(2)}) %copy-start) | copy-done | bytes 2328
  1.3 40.5 %shard_map.58 = (f32[16,32,256]{2,1,0:T(8,128)S(1)}, f32[8,128]{1,0:T(8,128)S(1)}) custom-call(f32[3,16,32,256]{3,2,1,0:T(8,128)} %disp.1, f32[16,32,256]{2,1,0:T(8,128)} %dens.1, f32[24,24]{1,0:T(8,128)S(1)} %copy-done), custom_call_target="tpu_custom_call" | custom-call | tf_op jit(solution)/shard_map/pallas_call | solution.py:547
  41.8 0.6 %fusion = (f32[1,1]{1,0:T(1,128)}, f32[1,1]{1,0:T(1,128)}) fusion(f32[8,128]{1,0:T(8,128)S(1)} %get-tuple-element.6), kind=kLoop, calls=%fused_computation | loop fusion | bytes 16 | tf_op jit(solution)/shard_map/slice | solution.py:588
  42.4 0.8 %copy.7 = f32[16,32,256]{2,1,0:T(8,128)} copy(f32[16,32,256]{2,1,0:T(8,128)S(1)} %get-tuple-element.12) | data formatting | bytes 1048576
Async XLA Ops:
  0.6 0.7 %copy-start = (f32[24,24]{1,0:T(8,128)S(1)}, f32[24,24]{1,0:T(8,128)}, u32[]{:S(2)}) copy-start(f32[24,24]{1,0:T(8,128)} %stiff.1) | copy-start | bytes 6916

commit v2 on v1

--- a/solution.py
+++ b/solution.py
@@ -16,7 +16,7 @@
 S_XYZ, S_RYZ = 16, 17
 N_SEM = 18
 GO_U, GO_R = 3, 4
-UNROLL_PREP, UNROLL_MAIN, UNROLL_LAST = 4, 7, 5
+UNROLL_LAST = 15
 
 
 def rounded(v):
@@ -61,6 +61,17 @@
             for cond, *actions in pairs:
                 when(cond, *actions)
 
+    loads = []
+    for t in range(2):
+        for m in range(3):
+            loads.append(pltpu.make_async_copy(
+                disp.at[m, :, :, pl.ds(128 * t, 128)], U.at[pl.ds(0, nx), m, t], load_sem.at[3 * t + m]))
+    for t in range(2):
+        loads.append(pltpu.make_async_copy(dens.at[:, :, pl.ds(128 * t, 128)], R.at[:, t], load_sem.at[6 + t]))
+    k_load = pltpu.make_async_copy(stiff, KV, load_sem.at[8])
+    for c in loads[:6] + [k_load]:
+        c.start()
+
     has_yl, has_yu = gy > 0, gy < py - 1
     has_zl, has_zu = gz > 0, gz < pz - 1
     last_x, first_x, upper0, lower1 = gx == px - 1, gx == 0, gx == half, gx == half - 1
@@ -78,21 +89,50 @@
     def as_int(c):
         return c.astype(jnp.int32)
 
-    key_x = xh * pz + gz
-    hy = py // 2
-    key_y = jnp.where(gy < hy, gy, py - 1 + hy - gy)
-    key_z = zc
-
-    def of_x(k):
-        return (k // pz) * half + zc, gy, k % pz
-
-    def of_y(k):
-        return gx, jnp.where(k < hy, k, py - 1 + hy - k), gz
-
-    def of_z(k):
-        return xh * half + k, gy, gz
-
-    groups = ((key_x, npz, of_x), (key_y, py, of_y), (key_z, half, of_z))
+    nxc, hx, hy = pz, pz // 2, py // 2
+    at_origin = lambda c: jnp.where(c, 1, 0)
+    ox = at_origin((gy == 0) & (zc == 0))
+    oy = at_origin((gx == 0) & (gz == 0))
+
+    def x_rank(x):
+        return jnp.where(x < hx, x, nxc - 1 + hx - x)
+
+    def y_rank(y):
+        return jnp.where(y < hy, y, py - 1 + hy - y)
+
+    my_x, core = xh * hx + gz // 2, gz % 2
+
+    def members_x():
+        for dx in (4, 3, 5, 2, 6, 1, 7, 0) if nxc == 8 else range(nxc):
+            for dc in range(2):
+                if dx or dc:
+                    x, c = (my_x + dx) % nxc, (core + dc) % 2
+                    yield key_of_x(x, c), ((x // hx) * half + zc, gy, 2 * (x % hx) + c)
+
+    def members_y():
+        for d in (4, 3, 5, 2, 6, 1, 7) if py == 8 else range(1, py):
+            y = (gy + d) % py
+            yield key_of_y(y), (gx, y, gz)
+
+    def members_z():
+        for d in range(1, half):
+            z = (zc + d) % half
+            yield z, (xh * half + z, gy, gz)
+
+    def key_of_x(x, c):
+        return (2 * x_rank(x) + 1 - c + npz - 2 * ox) % npz
+
+    def key_of_y(y):
+        return (y_rank(y) + py - oy) % py
+
+    groups = ((key_of_x(my_x, core), 2 * my_x + core, npz, members_x),
+              (key_of_y(gy), gy, py, members_y),
+              (zc, zc, half, members_z))
+
+    def send_go(slot):
+        key, _, _, members = groups[slot]
+        for other, place in members():
+            when(other < key, lambda: signal_go(slot, *place))
 
     when(has_zu, lambda: signal(gx, gy, gz + 1))
     when(has_zl, lambda: signal(gx, gy, gz - 1))
@@ -106,88 +146,36 @@
         when(cond & has_zu, lambda: signal(x, gy, gz + 1))
         when(cond & has_yu & has_zu, lambda: signal(x, gy + 1, gz + 1))
 
+    when(first_x, lambda: signal(half, gy, gz))
     edges(gx + 1, not_last & (gx != half - 1))
     edges(half, first_x)
-    for key, count, where_to in groups:
-        def tell(k, c, where_to=where_to):
-            signal(*where_to(k))
+    def of_x(k):
+        r = (k + 2 * ox) % npz
+        x = x_rank(r // 2)
+        return (x // hx) * half + zc, gy, 2 * (x % hx) + 1 - r % 2
+
+    def of_y(k):
+        return gx, y_rank((k + oy) % py), gz
+
+    def of_z(k):
+        return xh * half + k, gy, gz
+
+    for (key, _, count, _), place in zip(groups, (of_x, of_y, of_z)):
+        def tell(k, c, place=place):
+            signal(*place(k))
             return c
 
         lax.fori_loop(key + 1, count, tell, 0)
-    n_wait = as_int(has_zu) + as_int(has_zl) + as_int(has_yu) + as_int(has_yl) + as_int(has_yl & has_zl) + as_int(lower1)
-    n_wait = n_wait + key_x + key_y + key_z
+    n_wait = as_int(has_zu) + as_int(has_zl) + as_int(has_yu) + as_int(has_yl) + as_int(has_yl & has_zl) + as_int(lower1 | upper0)
+    n_wait = n_wait + groups[0][0] + groups[1][0] + groups[2][0]
     n_wait = n_wait + jnp.where(first_x, 0, as_int(has_yl) + as_int(has_zl) + as_int(has_yl & has_zl))
 
-    loads = []
-    for t in range(2):
-        for m in range(3):
-            loads.append(pltpu.make_async_copy(
-                disp.at[m, :, :, pl.ds(128 * t, 128)], U.at[pl.ds(0, nx), m, t], load_sem.at[3 * t + m]))
-    loads.append(pltpu.make_async_copy(stiff, KV, load_sem.at[8]))
-    for t in range(2):
-        loads.append(pltpu.make_async_copy(dens.at[:, :, pl.ds(128 * t, 128)], R.at[:, t], load_sem.at[6 + t]))
-    for c in loads:
+    for c in loads[6:]:
         c.start()
-
-    with jax.named_scope("w_bar"):
-        pl.semaphore_wait(bar, n_wait)
-    when(lower1, lambda: signal_go(GO_R, 0, gy, gz))
-
-    zero8 = jnp.zeros((8, 128), F32)
+    with jax.named_scope("w_bar0"):
+        when(lower1, lambda: pl.semaphore_wait(bar, n_wait), lambda: signal_go(GO_R, 0, gy, gz))
+
     zero32 = jnp.zeros((32, 128), F32)
-
-    @pl.when(last_x)
-    def _():
-        for m in range(3):
-            for t in range(2):
-                U[nx, m, t] = zero32
-        for t in range(2):
-            YH[t, nq:nq + 8, :] = zero8
-            F[nx + 2, t] = zero32
-            F[nx + 3, t] = zero32
-        ZX[1] = jnp.zeros((40, 128), F32)
-
-    @pl.when(first_x)
-    def _():
-        for t in range(2):
-            F[0, t] = zero32
-            F[1, t] = zero32
-
-    @pl.when(gy == py - 1)
-    def _():
-        for t in range(2):
-            YH[t] = jnp.zeros((nq + 8, 128), F32)
-            YR[1, t] = jnp.zeros((2 * nx, 128), F32)
-
-    @pl.when(gy == 0)
-    def _():
-        for t in range(2):
-            YR[0, t] = jnp.zeros((2 * nx, 128), F32)
-
-    @pl.when(gz == pz - 1)
-    def _():
-        ZX[0, 0:32, :] = zero32
-        ZX[1, 0:32, :] = zero32
-        CLr[...] = zero32
-
-    @pl.when((gz == pz - 1) | (gy == py - 1))
-    def _():
-        ZX[0, 32:40, :] = zero8
-        ZX[1, 32:40, :] = zero8
-
-    @pl.when(gz == 0)
-    def _():
-        CRr[...] = zero32
-
-    for t in range(2):
-        zr = lax.broadcasted_iota(jnp.int32, (256, 128), 0)
-        zl = lax.broadcasted_iota(jnp.int32, (256, 128), 1) + 128 * t
-        T[:, 128 * t:128 * t + 128] = jnp.maximum(3 - jnp.abs(zr - zl), 0).astype(F32).astype(jnp.bfloat16)
-        yv = lax.broadcasted_iota(jnp.int32, (32, 128), 0) + gy * ny
-        zv = lane32 + 128 * t + gz * 256
-        INV[t] = (F32(-3.0 * (1.0 - VOID)) * taps_sum(yv, py * ny)) * taps_sum(zv, pz * 256)
-    HR[...] = jnp.zeros(HR.shape, F32)
-
     with jax.named_scope("w_load0"):
         for c in loads[:3]:
             c.wait()
@@ -202,6 +190,9 @@
         for c in loads[3:6]:
             c.wait()
     YS[1] = Uf[pl.ds(32, nq, stride=64), :]
+
+    with jax.named_scope("w_bar"):
+        when(jnp.logical_not(lower1), lambda: pl.semaphore_wait(bar, n_wait))
 
     y_copy = remote(YS, YH.at[:, pl.ds(0, nq), :], S_Y, gx, gy - 1, gz)
     z_copy = remote(ZS, ZX.at[0, pl.ds(0, 32), :], S_Z, gx, gy, gz - 1)
@@ -232,7 +223,60 @@
     when(upper0 & has_zl, xz_to_relay.start)
     when(upper0 & both_l, xyz_to_relay.start)
 
-    loads[6].wait()
+    send_go(0)
+
+    zero8 = jnp.zeros((8, 128), F32)
+
+    @pl.when(last_x)
+    def _():
+        for m in range(3):
+            for t in range(2):
+                U[nx, m, t] = zero32
+        for t in range(2):
+            YH[t, nq:nq + 8, :] = zero8
+            F[nx + 2, t] = zero32
+            F[nx + 3, t] = zero32
+        ZX[1] = jnp.zeros((40, 128), F32)
+
+    @pl.when(first_x)
+    def _():
+        for t in range(2):
+            F[0, t] = zero32
+            F[1, t] = zero32
+
+    @pl.when(gy == py - 1)
+    def _():
+        for t in range(2):
+            YH[t] = jnp.zeros((nq + 8, 128), F32)
+            YR[1, t] = jnp.zeros((2 * nx, 128), F32)
+
+    @pl.when(gy == 0)
+    def _():
+        for t in range(2):
+            YR[0, t] = jnp.zeros((2 * nx, 128), F32)
+
+    @pl.when(gz == pz - 1)
+    def _():
+        ZX[0, 0:32, :] = zero32
+        ZX[1, 0:32, :] = zero32
+        CLr[...] = zero32
+
+    @pl.when((gz == pz - 1) | (gy == py - 1))
+    def _():
+        ZX[0, 32:40, :] = zero8
+        ZX[1, 32:40, :] = zero8
+
+    @pl.when(gz == 0)
+    def _():
+        CRr[...] = zero32
+
+    for t in range(2):
+        yv = lax.broadcasted_iota(jnp.int32, (32, 128), 0) + gy * ny
+        zv = lane32 + 128 * t + gz * 256
+        INV[t] = (F32(-3.0 * (1.0 - VOID)) * taps_sum(yv, py * ny)) * taps_sum(zv, pz * 256)
+    HR[...] = jnp.zeros(HR.shape, F32)
+
+    k_load.wait()
     kv = KV[...]
     k_hi = rounded(kv)
     k_lo = kv - k_hi
@@ -276,28 +320,16 @@
                 HR[p, t, 8 * j - 8 + 2 * m:8 * j - 7 + 2 * m, :] = x0[8 * j:8 * j + 1]
                 HR[p, t, 8 * j - 7 + 2 * m:8 * j - 6 + 2 * m, :] = x1[8 * j:8 * j + 1]
 
-    def prep(p, m, zx):
-        u0, u1 = U[p, m, 0], U[p, m, 1]
-        s0, s1 = pltpu.roll(u0, 127, 1), pltpu.roll(u1, 127, 1)
-        store_pair(p, m, 0, u0, jnp.where(lane32 == 127, s1, s0))
-        store_pair(p, m, 1, u1, jnp.where(lane32 == 127, zx, s1))
-
-    for slot, (key, count, where_to) in enumerate(groups):
-        def tell(k, c, slot=slot, where_to=where_to):
-            signal_go(slot, *where_to(k))
-            return c
-
-        lax.fori_loop(0, key, tell, 0)
-    when(zc > 0, lambda: signal_go(GO_U, gx - 1, gy, gz))
-
-    wait("w_z", (has_zu, z_copy.wait_recv))
-    with jax.named_scope("c_prep"):
-        def prep_planes(p, carry):
-            for m in range(3):
-                prep(p, m, pltpu.roll(ZX[0, 0:32, :], 127 - (3 * p + m), 1))
-            return carry
-
-        lax.fori_loop(0, nx, prep_planes, 0, unroll=UNROLL_PREP)
+    def shifted(p, m, t, zx):
+        s1 = pltpu.roll(U[p, m, 1], 127, 1)
+        if t == 1:
+            return jnp.where(lane32 == 127, zx, s1)
+        return jnp.where(lane32 == 127, s1, pltpu.roll(U[p, m, 0], 127, 1))
+
+    def prep(p, t, z_row=None, first=0):
+        for m in range(3):
+            zx = None if t == 0 else pltpu.roll(z_row, 127 - (3 * p + m - first), 1)
+            store_pair(p, m, t, U[p, m, t], shifted(p, m, t, zx))
 
     Gf = G.reshape(2 * (nx + 1) * 3 * 2 * 40, 128)
     HRf = HR.reshape((nx + 1) * 2 * 32, 128)
@@ -326,96 +358,112 @@
                     else:
                         HRf[pl.ds(at, planes, stride=64), :] = HY[c, t, pl.ds(first + m, planes, stride=3), :]
 
-    def blocks(i, js, acc):
+    def pairs(todo, acc):
         comp, vol = acc
-        rx = taps_sum(gx * nx + i, px * nx)
-        for j in js:
-            r0 = 8 * j
+        for pair in todo:
             cols = []
-            for t in range(2):
+            for i, j, t in pair:
                 tiles = [UH[i + a, m, t, j] for a in range(2) for m in range(3)]
-                tiles.append(jnp.concatenate([HR[i, t, r0:r0 + 8, :], HR[i + 1, t, r0:r0 + 8, :]], axis=0).astype(jnp.bfloat16))
+                tiles.append(jnp.concatenate(
+                    [HR[i, t, 8 * j:8 * j + 8, :], HR[i + 1, t, 8 * j:8 * j + 8, :]], axis=0).astype(jnp.bfloat16))
                 cols.append(jnp.concatenate(tiles, axis=0))
             rhs = jnp.concatenate(cols, axis=1)
             rhs = jnp.concatenate([rhs, rhs], axis=0)
             prod = jnp.dot(L[:, 0:224], rhs, preferred_element_type=F32)
-            for t in range(2):
+            for side, (i, j, t) in enumerate(pair):
+                r0 = 8 * j
                 e = None
                 for d in range(24):
                     m, a, b, c = d // 8, (d // 4) % 2, (d // 2) % 2, d % 2
-                    term = prod[8 * d:8 * d + 8, 128 * t:128 * t + 128] * G[c, i + a, m, t, pl.ds(r0 + b, 8), :]
+                    term = prod[8 * d:8 * d + 8, 128 * side:128 * side + 128] * G[c, i + a, m, t, pl.ds(r0 + b, 8), :]
                     e = term if e is None else e + term
                 rho = R[i, t, r0:r0 + 8, :]
                 r2 = rho * rho
                 comp = comp + (VOID + (r2 * rho) * (1.0 - VOID)) * e
                 vol = vol + rho
-                W[i, t, r0:r0 + 8, :] = (r2 * e) * (INV[t, r0:r0 + 8, :] * rx)
+                W[i, t, r0:r0 + 8, :] = (r2 * e) * (INV[t, r0:r0 + 8, :] * taps_sum(gx * nx + i, px * nx))
         return comp, vol
 
-    for c in loads[7:9]:
+    def half_region(t, z_row, acc):
+        for p in range(3):
+            prep(p, t, z_row)
+        for i in range(0, nx - 2, 2):
+            for p in (i + 3, i + 4):
+                if p < nx:
+                    prep(p, t, z_row)
+            acc = pairs([((i, 0, t), (i, 1, t)), ((i + 1, 0, t), (i + 1, 1, t)), ((i, 2, t), (i + 1, 2, t))], acc)
+        return acc
+
+    for c in loads[6:8]:
         c.wait()
-    first_part = (nx - 1) // 2
     with jax.named_scope("c_main0"):
-        acc = lax.fori_loop(0, first_part, lambda i, a: blocks(i, (0, 1, 2), a), (zero8, zero8), unroll=UNROLL_MAIN)
+        acc = half_region(0, None, (zero8, zero8))
+    wait("w_z", (has_zu, z_copy.wait_recv))
     with jax.named_scope("c_main1"):
-        acc = lax.fori_loop(first_part, nx - 1, lambda i, a: blocks(i, (0, 1, 2), a), acc, unroll=UNROLL_MAIN)
+        acc = half_region(1, ZX[0, 0:32, :], acc)
+        i = nx - 2
+        acc = pairs([((i, 0, 0), (i, 1, 0)), ((i, 0, 1), (i, 1, 1)), ((i, 2, 0), (i, 2, 1))], acc)
     wait("w_yz", (both_u, yz_copy.wait_recv))
     wait("w_y", (has_yu, y_copy.wait_recv))
     with jax.named_scope("c_halo"):
         halo_rows(0, nq, ZX[0, 32:33, :], nx)
     with jax.named_scope("c_main2"):
-        acc = lax.fori_loop(0, nx - 1, lambda i, a: blocks(i, (3,), a), acc, unroll=UNROLL_LAST)
+        acc = lax.fori_loop(0, nx - 1, lambda i, a: pairs([((i, 3, 0), (i, 3, 1))], a), acc, unroll=UNROLL_LAST)
 
     def relay():
         pl.semaphore_wait(go.at[GO_R], 1)
-        xm_to_relay.wait_recv()
-        xm_relay.start()
         when(has_yu, xy_to_relay.wait_recv, xy_relay.start)
         when(has_zu, xz_to_relay.wait_recv, xz_relay.start)
         when(both_u, xyz_to_relay.wait_recv, xyz_relay.start)
+        xm_to_relay.wait_recv()
+        xm_relay.start()
 
     wait("w_xm", (not_last, xm_copy.wait_recv))
     wait("w_xe", (not_last & has_yu, xy_copy.wait_recv), (not_last & has_zu, xz_copy.wait_recv),
          (not_last & both_u, xyz_copy.wait_recv))
     with jax.named_scope("c_last"):
-        for m in range(3):
-            prep(nx, m, pltpu.roll(ZX[1, 0:32, :], 127 - m, 1))
+        prep(nx, 0)
+        prep(nx, 1, ZX[1, 0:32, :], 3 * nx)
         halo_rows(nq, 8, ZX[1, 32:33, :], 1)
-        comp, vol = blocks(nx - 1, (0, 1, 2, 3), acc)
-
-    def stage_send(buf, stage):
-        key, count, where_to = groups[stage]
+        i = nx - 1
+        comp, vol = pairs([((i, j, 0), (i, j, 1)) for j in range(4)], acc)
+
+    def stage_send(buf, stage, row):
+        key, me, count, members = groups[stage]
+        buf[me] = row
         with jax.named_scope(f"w_go{stage}"):
             when(key < count - 1, lambda: pl.semaphore_wait(go.at[stage], count - 1 - key))
-
-        def send(k, c):
+        for _, place in members():
             pltpu.make_async_remote_copy(
-                src_ref=buf.at[key], dst_ref=buf.at[key], send_sem=ar_send.at[stage], recv_sem=ar_recv.at[stage],
-                device_id=dev(*where_to(k)), device_id_type=MESH).start()
-            return c
-
-        lax.fori_loop(0, key, send, 0)
-        lax.fori_loop(key + 1, count, send, 0)
+                src_ref=buf.at[me], dst_ref=buf.at[me], send_sem=ar_send.at[stage], recv_sem=ar_recv.at[stage],
+                device_id=dev(*place), device_id_type=MESH).start()
 
     def stage_wait(buf, stage):
-        count = groups[stage][1]
+        count = groups[stage][2]
         part = buf.at[pl.ds(0, count - 1)]
         with jax.named_scope(f"w_ar{stage}"):
             pltpu.make_async_copy(part, part, ar_recv.at[stage]).wait()
-        total = buf[0]
-        for k in range(1, count):
-            total = total + buf[k]
-        return total
+        rows = [buf[k] for k in range(count)]
+        while len(rows) > 1:
+            rows = [a + b for a, b in zip(rows[::2], rows[1::2])]
+        return rows[0]
 
     def stage_done(buf, stage):
-        part = buf.at[pl.ds(0, groups[stage][1] - 1)]
+        part = buf.at[pl.ds(0, groups[stage][2] - 1)]
         pltpu.make_async_copy(part, part, ar_send.at[stage]).wait()
 
     lane1 = lax.broadcasted_iota(jnp.int32, (1, 128), 1)
     comp_all = jnp.sum(jnp.sum(comp, axis=0, keepdims=True), axis=1, keepdims=True)
     vol_all = jnp.sum(jnp.sum(vol, axis=0, keepdims=True), axis=1, keepdims=True)
-    A1[key_x] = jnp.where(lane1 == 0, jnp.broadcast_to(comp_all, (1, 128)), jnp.broadcast_to(vol_all, (1, 128)))
-    stage_send(A1, 0)
+    stage_send(A1, 0, jnp.where(lane1 == 0, jnp.broadcast_to(comp_all, (1, 128)), jnp.broadcast_to(vol_all, (1, 128))))
+    send_go(1)
+    send_go(2)
+    when(zc > 0, lambda: signal_go(GO_U, gx - 1, gy, gz))
+
+    for t in range(2):
+        zr = lax.broadcasted_iota(jnp.int32, (256, 128), 0)
+        zl = lax.broadcasted_iota(jnp.int32, (256, 128), 1) + 128 * t
+        T[:, 128 * t:128 * t + 128] = jnp.maximum(3 - jnp.abs(zr - zl), 0).astype(F32).astype(jnp.bfloat16)
 
     with jax.named_scope("c_packw"):
         lo, hi = zero32, zero32
@@ -463,9 +511,7 @@
     when(has_yl, yd_copy.start)
     when(has_yu, yu_copy.start)
 
-    total = stage_wait(A1, 0)
-    A2[key_y] = total
-    stage_send(A2, 1)
+    stage_send(A2, 1, stage_wait(A1, 0))
 
     wait("w_wy", (has_yu, yd_copy.wait_recv), (has_yl, yu_copy.wait_recv))
     for t in range(2):
@@ -500,9 +546,7 @@
     wait("w_frelay", (first_x, xd_to_relay.wait_recv, xd_relay.start))
     with jax.named_scope("c_fx"):
         lax.fori_loop(2, nx - 2, filter_x, 0, unroll=2)
-    total = stage_wait(A2, 1)
-    A3[key_z] = total
-    stage_send(A3, 2)
+    stage_send(A3, 2, stage_wait(A2, 1))
 
     wait("w_fd", (not_last, xd_copy.wait_recv))
     for p in (nx - 2, nx - 1):
@@ -537,6 +581,18 @@
     total = stage_wait(A3, 2)
     count = F32(px * nx) * F32(py * ny) * F32(pz * 256)
     sums[...] = jnp.broadcast_to(total / count, (8, 128))
+
+
+def finish(out_ref, sums_ref, filtered, comp, vol, c_ref, v_ref, sem):
+    copies = [pltpu.make_async_copy(out_ref, filtered, sem.at[0])]
+    copies[0].start()
+    c_ref[...] = sums_ref[0:1, 0:1]
+    v_ref[...] = sums_ref[0:1, 1:2]
+    for k, (src, dst) in enumerate(((c_ref, comp), (v_ref, vol))):
+        copies.append(pltpu.make_async_copy(src, dst, sem.at[1 + k]))
+        copies[-1].start()
+    for c in copies:
+        c.wait()
 
 
 def on_device(displacement, density, stiffness):
@@ -584,8 +640,17 @@
             pltpu.SemaphoreType.REGULAR((5,)),
         ],
         compiler_params=pltpu.CompilerParams(collective_id=0, has_side_effects=True, vmem_limit_bytes=56_000_000),
-    )(displacement, density, stiffness)
-    return out, sums[0, 0], sums[0, 1]
+    )(displacement, density, pltpu.with_memory_space_constraint(stiffness, pltpu.HBM))
+    vmem = pl.BlockSpec(memory_space=pltpu.VMEM)
+    out, comp, vol = pl.pallas_call(
+        finish,
+        out_shape=(jax.ShapeDtypeStruct((nx, ny, nz), F32), jax.ShapeDtypeStruct((1, 1), F32), jax.ShapeDtypeStruct((1, 1), F32)),
+        in_specs=[vmem, vmem],
+        out_specs=(pl.BlockSpec(memory_space=pltpu.HBM),) * 3,
+        scratch_shapes=[pltpu.VMEM((1, 1), F32), pltpu.VMEM((1, 1), F32), pltpu.SemaphoreType.DMA((3,))],
+        compiler_params=pltpu.CompilerParams(vmem_limit_bytes=4 << 20),
+    )(out, sums)
+    return out, comp.reshape(()), vol.reshape(())
 
 
 def solution(mesh):

time: 43.4 us -> 41.3 us (0.952)
  the two profiles are of different devices: /device:TPU:4 before, /device:TPU:2 now
where the time goes in v2:
time: 41.3 us; the launch traced here: 41.1 us
  Pallas kernels  40.5 us (98%)
  between operations  0.64 us (2%)
    pallas_call x1, Pallas kernels, on_device(): pl.pallas_call(functools.partial(kernel, nx, ny, px, py, pz), out_shape=(...  39.7 us

profile of v2, /device:TPU:2, one launch (start us, length us, event | category | flops | bytes accessed | tf_op | source)
XLA Modules:
  0.0 41.1 jit_solution(16851515684576924491)
XLA Ops:
  0.6 39.7 %shard_map.58 = (f32[16,32,256]{2,1,0:T(8,128)S(1)}, f32[8,128]{1,0:T(8,128)S(1)}) custom-call(f32[3,16,32,256]{3,2,1,0:T(8,128)} %disp.1, f32[16,32,256]{2,1,0:T(8,128)} %dens.1, f32[24,24]{1,0:T(8,128)} %stiff.1), custom_call_target="tpu_custom_call" | custom-call | tf_op jit(solution)/shard_map/pallas_call | solution.py:603
  40.3 0.8 %shard_map.59 = (f32[16,32,256]{2,1,0:T(8,128)}, f32[1,1]{1,0:T(1,128)}, f32[1,1]{1,0:T(1,128)}) custom-call(f32[16,32,256]{2,1,0:T(8,128)S(1)} %get-tuple-element.8.out_ref, f32[8,128]{1,0:T(8,128)S(1)} %get-tuple-element.9.sums_ref), custom_call_target="tpu_custom_call" | custom-call | tf_op jit(solution)/shard_map/pallas_call | solution.py:645

commit v3 on v2

--- a/solution.py
+++ b/solution.py
@@ -15,7 +15,7 @@
 S_ZL, S_ZR, S_YD, S_YU, S_XD, S_XU, S_RF = range(9, 16)
 S_XYZ, S_RYZ = 16, 17
 N_SEM = 18
-GO_U, GO_R = 3, 4
+GO_U, GO_R, GO_T = 3, 4, 5
 UNROLL_LAST = 15
 
 
@@ -34,7 +34,7 @@
            U, UH, G, HR, R, W, Z, F, T, L, KV, INV,
            YS, YH, HY, GY, ZS, ZX, RU, RY, RZ,
            CL, CR, CLr, CRr, YS2, YR, RF, A1, A2, A3,
-           load_sem, send_sem, recv_sem, ar_send, ar_recv, go):
+           load_sem, send_sem, recv_sem, ar_send, ar_recv, down_send, down_recv, up_send, up_recv, go):
     gx, gy, gz = lax.axis_index("gx"), lax.axis_index("gy"), lax.axis_index("gz")
     half = px // 2
     xh, zc = gx // half, gx % half
@@ -224,6 +224,7 @@
     when(upper0 & both_l, xyz_to_relay.start)
 
     send_go(0)
+    send_go(1)
 
     zero8 = jnp.zeros((8, 128), F32)
 
@@ -428,36 +429,47 @@
         i = nx - 1
         comp, vol = pairs([((i, j, 0), (i, j, 1)) for j in range(4)], acc)
 
-    def stage_send(buf, stage, row):
-        key, me, count, members = groups[stage]
-        buf[me] = row
-        with jax.named_scope(f"w_go{stage}"):
-            when(key < count - 1, lambda: pl.semaphore_wait(go.at[stage], count - 1 - key))
-        for _, place in members():
-            pltpu.make_async_remote_copy(
-                src_ref=buf.at[me], dst_ref=buf.at[me], send_sem=ar_send.at[stage], recv_sem=ar_recv.at[stage],
-                device_id=dev(*place), device_id_type=MESH).start()
-
-    def stage_wait(buf, stage):
-        count = groups[stage][2]
-        part = buf.at[pl.ds(0, count - 1)]
-        with jax.named_scope(f"w_ar{stage}"):
-            pltpu.make_async_copy(part, part, ar_recv.at[stage]).wait()
-        rows = [buf[k] for k in range(count)]
+    row_of = zc * py + gy
+
+    def row_copy(buf, me, sems, place):
+        return pltpu.make_async_remote_copy(
+            src_ref=buf.at[me], dst_ref=buf.at[me], send_sem=sems[0], recv_sem=sems[1],
+            device_id=dev(*place), device_id_type=MESH)
+
+    def wait_rows(buf, count, sem):
+        part = buf.at[pl.ds(0, count)]
+        pltpu.make_async_copy(part, part, sem).wait()
+
+    def add_up(rows):
         while len(rows) > 1:
-            rows = [a + b for a, b in zip(rows[::2], rows[1::2])]
+            rows = [a + b for a, b in zip(rows[::2], rows[1::2])] + ([rows[-1]] if len(rows) % 2 else [])
         return rows[0]
 
-    def stage_done(buf, stage):
-        part = buf.at[pl.ds(0, groups[stage][2] - 1)]
-        pltpu.make_async_copy(part, part, ar_send.at[stage]).wait()
+    def x_copy(place):
+        return row_copy(A1, groups[0][1], (ar_send.at[0], ar_recv.at[0]), place)
+
+    def y_copy_of(place):
+        return row_copy(A2, row_of, (ar_send.at[1], ar_recv.at[1]), place)
+
+    def down_copy(z, y):
+        return row_copy(A2, row_of, (down_send.at[z], down_recv.at[zc]), (xh * half + z, y, gz))
+
+    def up_copy(z):
+        return row_copy(A3, zc, (up_send.at[z], up_recv.at[zc]), (xh * half + z, gy, gz))
+
+    def when_any(number, slot):
+        when(number > 0, lambda: pl.semaphore_wait(go.at[slot], number))
+
+    key_y = groups[1][0]
 
     lane1 = lax.broadcasted_iota(jnp.int32, (1, 128), 1)
     comp_all = jnp.sum(jnp.sum(comp, axis=0, keepdims=True), axis=1, keepdims=True)
     vol_all = jnp.sum(jnp.sum(vol, axis=0, keepdims=True), axis=1, keepdims=True)
-    stage_send(A1, 0, jnp.where(lane1 == 0, jnp.broadcast_to(comp_all, (1, 128)), jnp.broadcast_to(vol_all, (1, 128))))
-    send_go(1)
-    send_go(2)
+    A1[groups[0][1]] = jnp.where(lane1 == 0, jnp.broadcast_to(comp_all, (1, 128)), jnp.broadcast_to(vol_all, (1, 128)))
+    with jax.named_scope("w_go0"):
+        when_any(npz - 1 - groups[0][0], 0)
+    for _, place in members_x():
+        x_copy(place).start()
     when(zc > 0, lambda: signal_go(GO_U, gx - 1, gy, gz))
 
     for t in range(2):
@@ -493,6 +505,11 @@
     with jax.named_scope("c_fz"):
         lax.fori_loop(0, nx // 4, filter_z, 0, unroll=True)
 
+    with jax.named_scope("w_go1"):
+        when_any(py - 1 - key_y, 1)
+    for other, place in members_y():
+        when(other > key_y, lambda: signal_go(GO_T, *place))
+    send_go(2)
     wait("w_relay", (first_x, relay))
     wait("w_wz", (has_zu, zl_copy.wait_recv), (has_zl, zr_copy.wait_recv))
     with jax.named_scope("c_fixz"):
@@ -511,7 +528,22 @@
     when(has_yl, yd_copy.start)
     when(has_yu, yu_copy.start)
 
-    stage_send(A2, 1, stage_wait(A1, 0))
+    def second_stage():
+        with jax.named_scope("w_ar0"):
+            wait_rows(A1, npz - 1, ar_recv.at[0])
+        A2[row_of] = add_up([A1[k] for k in range(npz)])
+        with jax.named_scope("w_got"):
+            when_any(key_y, GO_T)
+        for z in range(half - 1):
+            @pl.when(z < zc)
+            def _():
+                for dy in range(py):
+                    down_copy(z, (gy + hy + dy) % py).start()
+        for _, place in members_y():
+            y_copy_of(place).start()
+
+    layers_first = lower1 & (gy == 0)
+    when(jnp.logical_not(layers_first), second_stage)
 
     wait("w_wy", (has_yu, yd_copy.wait_recv), (has_yl, yu_copy.wait_recv))
     for t in range(2):
@@ -536,6 +568,7 @@
     when(upper0, xd_to_relay.start)
     when(zc < half - 1, lambda: pl.semaphore_wait(go.at[GO_U], 1))
     when(not_last, xu_copy.start)
+    when(layers_first, second_stage)
 
     def filter_x(p, carry):
         for t in range(2):
@@ -546,7 +579,13 @@
     wait("w_frelay", (first_x, xd_to_relay.wait_recv, xd_relay.start))
     with jax.named_scope("c_fx"):
         lax.fori_loop(2, nx - 2, filter_x, 0, unroll=2)
-    stage_send(A3, 2, stage_wait(A2, 1))
+    with jax.named_scope("w_ar1"):
+        wait_rows(A2, py - 1, ar_recv.at[1])
+    A3[zc] = add_up([A2[zc * py + k] for k in range(py)])
+    with jax.named_scope("w_go2"):
+        when_any(half - 1 - zc, 2)
+    for z in range(1, half):
+        when(z > zc, up_copy(z).start)
 
     wait("w_fd", (not_last, xd_copy.wait_recv))
     for p in (nx - 2, nx - 1):
@@ -574,11 +613,25 @@
         when(first_x & has_zu, xz_relay.wait_send)
         when(first_x & both_u, xyz_relay.wait_send)
         when(not_last, xu_copy.wait_send)
-        stage_done(A1, 0)
-        stage_done(A2, 1)
-        stage_done(A3, 2)
-
-    total = stage_wait(A3, 2)
+        wait_rows(A1, npz - 1, ar_send.at[0])
+        wait_rows(A2, py - 1, ar_send.at[1])
+        for z in range(half):
+            when(z < zc, lambda: wait_rows(A2, py, down_send.at[z]))
+            when(z > zc, lambda: wait_rows(A3, 1, up_send.at[z]))
+
+    def add_upper(z, c):
+        wait_rows(A2, py, down_recv.at[z])
+        A3[z] = add_up([A2[z * py + k] for k in range(py)])
+        return c
+
+    def add_lower(z, c):
+        wait_rows(A3, 1, up_recv.at[z])
+        return c
+
+    with jax.named_scope("w_ar2"):
+        lax.fori_loop(0, zc, add_lower, 0)
+        lax.fori_loop(zc + 1, half, add_upper, 0)
+    total = add_up([A3[z] for z in range(half)])
     count = F32(px * nx) * F32(py * ny) * F32(pz * 256)
     sums[...] = jnp.broadcast_to(total / count, (8, 128))
 
@@ -631,13 +684,17 @@
             vm(2, 2, 2 * nx, 128),
             vm(2, 2, 2 * nx, 128),
             vm(2, 2, 32, 128),
-            vm(2 * pz, 1, 128), vm(py, 1, 128), vm(px // 2, 1, 128),
+            vm(2 * pz, 1, 128), vm(py * px // 2, 1, 128), vm(px // 2, 1, 128),
             pltpu.SemaphoreType.DMA((9,)),
             pltpu.SemaphoreType.DMA((N_SEM,)),
             pltpu.SemaphoreType.DMA((N_SEM,)),
-            pltpu.SemaphoreType.DMA((3,)),
-            pltpu.SemaphoreType.DMA((3,)),
-            pltpu.SemaphoreType.REGULAR((5,)),
+            pltpu.SemaphoreType.DMA((2,)),
+            pltpu.SemaphoreType.DMA((2,)),
+            pltpu.SemaphoreType.DMA((px // 2,)),
+            pltpu.SemaphoreType.DMA((px // 2,)),
+            pltpu.SemaphoreType.DMA((px // 2,)),
+            pltpu.SemaphoreType.DMA((px // 2,)),
+            pltpu.SemaphoreType.REGULAR((6,)),
         ],
         compiler_params=pltpu.CompilerParams(collective_id=0, has_side_effects=True, vmem_limit_bytes=56_000_000),
     )(displacement, density, pltpu.with_memory_space_constraint(stiffness, pltpu.HBM))

time: 41.3 us -> 40 us (0.969)
  the two profiles are of different devices: /device:TPU:2 before, /device:TPU:1 now
where the time goes in v3:
time: 40 us; the launch traced here: 39.5 us
  Pallas kernels  38.8 us (97%)
  between operations  0.64 us (2%)
    pallas_call x1, Pallas kernels, on_device(): pl.pallas_call(functools.partial(kernel, nx, ny, px, py, pz), out_shape=(...  38 us
    pallas_call x1, Pallas kernels, on_device(): pl.pallas_call(finish, out_shape=(jax.ShapeDtypeStruct((nx, ny, nz), F32)...  0.83 us

profile of v3, /device:TPU:1, one launch (start us, length us, event | category | flops | bytes accessed | tf_op | source)
XLA Modules:
  0.0 39.5 jit_solution(12533981989226833317)
XLA Ops:
  0.6 38.0 %shard_map.58 = (f32[16,32,256]{2,1,0:T(8,128)S(1)}, f32[8,128]{1,0:T(8,128)S(1)}) custom-call(f32[3,16,32,256]{3,2,1,0:T(8,128)} %disp.1, f32[16,32,256]{2,1,0:T(8,128)} %dens.1, f32[24,24]{1,0:T(8,128)} %stiff.1), custom_call_target="tpu_custom_call" | custom-call | tf_op jit(solution)/shard_map/pallas_call | solution.py:656
  38.6 0.8 %shard_map.59 = (f32[16,32,256]{2,1,0:T(8,128)}, f32[1,1]{1,0:T(1,128)}, f32[1,1]{1,0:T(1,128)}) custom-call(f32[16,32,256]{2,1,0:T(8,128)S(1)} %get-tuple-element.8.out_ref, f32[8,128]{1,0:T(8,128)S(1)} %get-tuple-element.9.sums_ref), custom_call_target="tpu_custom_call" | custom-call | tf_op jit(solution)/shard_map/pallas_call | solution.py:702

commit v4 on v3

--- a/solution.py
+++ b/solution.py
@@ -15,7 +15,7 @@
 S_ZL, S_ZR, S_YD, S_YU, S_XD, S_XU, S_RF = range(9, 16)
 S_XYZ, S_RYZ = 16, 17
 N_SEM = 18
-GO_U, GO_R, GO_T = 3, 4, 5
+GO_U, GO_R, GO_T, GO_V = 3, 4, 5, 6
 UNROLL_LAST = 15
 
 
@@ -137,7 +137,6 @@
     when(has_zu, lambda: signal(gx, gy, gz + 1))
     when(has_zl, lambda: signal(gx, gy, gz - 1))
     when(has_yu, lambda: signal(gx, gy + 1, gz))
-    when(has_yl, lambda: signal(gx, gy - 1, gz))
     when(has_yu & has_zu, lambda: signal(gx, gy + 1, gz + 1))
     when(upper0, lambda: signal(half - 1, gy, gz))
 
@@ -148,7 +147,10 @@
 
     when(first_x, lambda: signal(half, gy, gz))
     edges(gx + 1, not_last & (gx != half - 1))
-    edges(half, first_x)
+    edges(half, first_x & ((gy > 0) | (gz > 0)))
+    skip_y, skip_z, skip_yz = (upper0 & (gy == y) & (gz == z) for y, z in ((1, 0), (0, 1), (1, 1)))
+    at_corner = upper0 & (gy == 0) & (gz == 0)
+    when((gx == half + half // 2 - 1) & (gy < 2) & (gz < 2) & (gy + gz > 0), lambda: signal(half, gy, gz))
     def of_x(k):
         r = (k + 2 * ox) % npz
         x = x_rank(r // 2)
@@ -166,7 +168,7 @@
             return c
 
         lax.fori_loop(key + 1, count, tell, 0)
-    n_wait = as_int(has_zu) + as_int(has_zl) + as_int(has_yu) + as_int(has_yl) + as_int(has_yl & has_zl) + as_int(lower1 | upper0)
+    n_wait = as_int(has_zu) + as_int(has_zl) + as_int(has_yl) + as_int(has_yl & has_zl) + as_int(lower1 | upper0)
     n_wait = n_wait + groups[0][0] + groups[1][0] + groups[2][0]
     n_wait = n_wait + jnp.where(first_x, 0, as_int(has_yl) + as_int(has_zl) + as_int(has_yl & has_zl))
 
@@ -219,10 +221,15 @@
     when(plain_down & has_yl, xy_copy.start)
     when(plain_down & has_zl, xz_copy.start)
     when(plain_down & both_l, xyz_copy.start)
-    when(upper0 & has_yl, xy_to_relay.start)
-    when(upper0 & has_zl, xz_to_relay.start)
-    when(upper0 & both_l, xyz_to_relay.start)
-
+    no = jnp.logical_not
+    when(upper0 & has_yl & no(skip_y), xy_to_relay.start)
+    when(upper0 & has_zl & no(skip_z), xz_to_relay.start)
+    when(upper0 & both_l & no(skip_yz), xyz_to_relay.start)
+    xy_corner = remote(YH.at[:, pl.ds(0, 8), :], RY, S_RY, 0, gy, gz)
+    xz_corner = remote(ZX.at[0, pl.ds(0, 32), :], RZ.at[pl.ds(0, 32), :], S_RZ, 0, gy, gz)
+    xyz_corner = remote(ZX.at[0, pl.ds(32, 8), :], RZ.at[pl.ds(32, 8), :], S_RYZ, 0, gy, gz)
+
+    when(has_yl, lambda: signal_go(GO_V, gx, gy - 1, gz))
     send_go(0)
     send_go(1)
 
@@ -406,6 +413,9 @@
         acc = pairs([((i, 0, 0), (i, 1, 0)), ((i, 0, 1), (i, 1, 1)), ((i, 2, 0), (i, 2, 1))], acc)
     wait("w_yz", (both_u, yz_copy.wait_recv))
     wait("w_y", (has_yu, y_copy.wait_recv))
+    when(at_corner & has_yu, xy_corner.start)
+    when(at_corner & has_zu, xz_corner.start)
+    when(at_corner & both_u, xyz_corner.start)
     with jax.named_scope("c_halo"):
         halo_rows(0, nq, ZX[0, 32:33, :], nx)
     with jax.named_scope("c_main2"):
@@ -466,6 +476,7 @@
     comp_all = jnp.sum(jnp.sum(comp, axis=0, keepdims=True), axis=1, keepdims=True)
     vol_all = jnp.sum(jnp.sum(vol, axis=0, keepdims=True), axis=1, keepdims=True)
     A1[groups[0][1]] = jnp.where(lane1 == 0, jnp.broadcast_to(comp_all, (1, 128)), jnp.broadcast_to(vol_all, (1, 128)))
+    wait("w_relay", (first_x, relay))
     with jax.named_scope("w_go0"):
         when_any(npz - 1 - groups[0][0], 0)
     for _, place in members_x():
@@ -510,7 +521,6 @@
     for other, place in members_y():
         when(other > key_y, lambda: signal_go(GO_T, *place))
     send_go(2)
-    wait("w_relay", (first_x, relay))
     wait("w_wz", (has_zu, zl_copy.wait_recv), (has_zl, zr_copy.wait_recv))
     with jax.named_scope("c_fixz"):
         left, right = CRr[...], CLr[...]
@@ -526,7 +536,7 @@
     yd_copy = remote(YS2.at[0], YR.at[1], S_YD, gx, gy - 1, gz)
     yu_copy = remote(YS2.at[1], YR.at[0], S_YU, gx, gy + 1, gz)
     when(has_yl, yd_copy.start)
-    when(has_yu, yu_copy.start)
+    when(has_yu, lambda: pl.semaphore_wait(go.at[GO_V], 1), yu_copy.start)
 
     def second_stage():
         with jax.named_scope("w_ar0"):
@@ -605,9 +615,12 @@
         when(plain_down & has_zl, xz_copy.wait_send)
         when(plain_down & both_l, xyz_copy.wait_send)
         when(upper0, xm_to_relay.wait_send, xd_to_relay.wait_send)
-        when(upper0 & has_yl, xy_to_relay.wait_send)
-        when(upper0 & has_zl, xz_to_relay.wait_send)
-        when(upper0 & both_l, xyz_to_relay.wait_send)
+        when(upper0 & has_yl & no(skip_y), xy_to_relay.wait_send)
+        when(upper0 & has_zl & no(skip_z), xz_to_relay.wait_send)
+        when(upper0 & both_l & no(skip_yz), xyz_to_relay.wait_send)
+        when(at_corner & has_yu, xy_corner.wait_send)
+        when(at_corner & has_zu, xz_corner.wait_send)
+        when(at_corner & both_u, xyz_corner.wait_send)
         when(first_x, xm_relay.wait_send, xd_relay.wait_send)
         when(first_x & has_yu, xy_relay.wait_send)
         when(first_x & has_zu, xz_relay.wait_send)
@@ -694,7 +707,7 @@
             pltpu.SemaphoreType.DMA((px // 2,)),
             pltpu.SemaphoreType.DMA((px // 2,)),
             pltpu.SemaphoreType.DMA((px // 2,)),
-            pltpu.SemaphoreType.REGULAR((6,)),
+            pltpu.SemaphoreType.REGULAR((7,)),
         ],
         compiler_params=pltpu.CompilerParams(collective_id=0, has_side_effects=True, vmem_limit_bytes=56_000_000),
     )(displacement, density, pltpu.with_memory_space_constraint(stiffness, pltpu.HBM))

time: 40 us -> 39.9 us (level)
  no operation moved by 1% of the time
where the time goes in v4:
time: 39.9 us; the launch traced here: 39.5 us
  Pallas kernels  38.8 us (97%)
  between operations  0.64 us (2%)
    pallas_call x1, Pallas kernels, on_device(): pl.pallas_call(functools.partial(kernel, nx, ny, px, py, pz), out_shape=(...  38 us
    pallas_call x1, Pallas kernels, on_device(): pl.pallas_call(finish, out_shape=(jax.ShapeDtypeStruct((nx, ny, nz), F32)...  0.83 us

profile of v4, /device:TPU:1, one launch (start us, length us, event | category | flops | bytes accessed | tf_op | source)
XLA Modules:
  0.0 39.5 jit_solution(4669867389428328348)
XLA Ops:
  0.6 38.0 %shard_map.58 = (f32[16,32,256]{2,1,0:T(8,128)S(1)}, f32[8,128]{1,0:T(8,128)S(1)}) custom-call(f32[3,16,32,256]{3,2,1,0:T(8,128)} %disp.1, f32[16,32,256]{2,1,0:T(8,128)} %dens.1, f32[24,24]{1,0:T(8,128)} %stiff.1), custom_call_target="tpu_custom_call" | custom-call | tf_op jit(solution)/shard_map/pallas_call | solution.py:669
  38.7 0.8 %shard_map.59 = (f32[16,32,256]{2,1,0:T(8,128)}, f32[1,1]{1,0:T(1,128)}, f32[1,1]{1,0:T(1,128)}) custom-call(f32[16,32,256]{2,1,0:T(8,128)S(1)} %get-tuple-element.8.out_ref, f32[8,128]{1,0:T(8,128)S(1)} %get-tuple-element.9.sums_ref), custom_call_target="tpu_custom_call" | custom-call | tf_op jit(solution)/shard_map/pallas_call | solution.py:715

commit v5 on v4

--- a/solution.py
+++ b/solution.py
@@ -14,7 +14,8 @@
 S_Y, S_Z, S_YZ, S_XM, S_XY, S_XZ, S_RM, S_RY, S_RZ = range(9)
 S_ZL, S_ZR, S_YD, S_YU, S_XD, S_XU, S_RF = range(9, 16)
 S_XYZ, S_RYZ = 16, 17
-N_SEM = 18
+S_HALF = 15
+N_SEM = 22
 GO_U, GO_R, GO_T, GO_V = 3, 4, 5, 6
 UNROLL_LAST = 15
 
@@ -162,7 +163,7 @@
     def of_z(k):
         return xh * half + k, gy, gz
 
-    for (key, _, count, _), place in zip(groups, (of_x, of_y, of_z)):
+    for (key, _, count, _), place in zip((groups[1], groups[2], groups[0]), (of_y, of_z, of_x)):
         def tell(k, c, place=place):
             signal(*place(k))
             return c
@@ -199,9 +200,10 @@
     y_copy = remote(YS, YH.at[:, pl.ds(0, nq), :], S_Y, gx, gy - 1, gz)
     z_copy = remote(ZS, ZX.at[0, pl.ds(0, 32), :], S_Z, gx, gy, gz - 1)
     yz_copy = remote(ZS.at[pl.ds(0, 8), :], ZX.at[0, pl.ds(32, 8), :], S_YZ, gx, gy - 1, gz - 1)
-    xm_copy = remote(U.at[0], U.at[nx], S_XM, gx - 1, gy, gz)
-    xm_to_relay = remote(U.at[0], RU, S_RM, 0, gy, gz)
-    xm_relay = remote(RU, U.at[nx], S_XM, half - 1, gy, gz)
+    xm_copy, xm_to_relay, xm_relay = ([f(t) for t in range(2)] for f in (
+        lambda t: remote(U.at[0, :, t], U.at[nx, :, t], S_XM + t * S_HALF, gx - 1, gy, gz),
+        lambda t: remote(U.at[0, :, t], RU.at[:, t], S_RM + t * S_HALF, 0, gy, gz),
+        lambda t: remote(RU.at[:, t], U.at[nx, :, t], S_XM + t * S_HALF, half - 1, gy, gz)))
     xy_copy = remote(YS.at[:, pl.ds(0, 8), :], YH.at[:, pl.ds(nq, 8), :], S_XY, gx - 1, gy - 1, gz)
     xy_to_relay = remote(YS.at[:, pl.ds(0, 8), :], RY, S_RY, 0, gy - 1, gz)
     xy_relay = remote(RY, YH.at[:, pl.ds(nq, 8), :], S_XY, half - 1, gy, gz)
@@ -216,8 +218,8 @@
     when(has_zl, z_copy.start)
     when(has_yl & has_zl, yz_copy.start)
     when(has_yl, y_copy.start)
-    when(plain_down, xm_copy.start)
-    when(upper0, xm_to_relay.start)
+    when(plain_down, xm_copy[1].start, xm_copy[0].start)
+    when(upper0, xm_to_relay[1].start, xm_to_relay[0].start)
     when(plain_down & has_yl, xy_copy.start)
     when(plain_down & has_zl, xz_copy.start)
     when(plain_down & both_l, xyz_copy.start)
@@ -426,18 +428,20 @@
         when(has_yu, xy_to_relay.wait_recv, xy_relay.start)
         when(has_zu, xz_to_relay.wait_recv, xz_relay.start)
         when(both_u, xyz_to_relay.wait_recv, xyz_relay.start)
-        xm_to_relay.wait_recv()
-        xm_relay.start()
-
-    wait("w_xm", (not_last, xm_copy.wait_recv))
+        for t in (1, 0):
+            xm_to_relay[t].wait_recv()
+            xm_relay[t].start()
+
     wait("w_xe", (not_last & has_yu, xy_copy.wait_recv), (not_last & has_zu, xz_copy.wait_recv),
          (not_last & both_u, xyz_copy.wait_recv))
-    with jax.named_scope("c_last"):
-        prep(nx, 0)
-        prep(nx, 1, ZX[1, 0:32, :], 3 * nx)
-        halo_rows(nq, 8, ZX[1, 32:33, :], 1)
-        i = nx - 1
-        comp, vol = pairs([((i, j, 0), (i, j, 1)) for j in range(4)], acc)
+    i = nx - 1
+    halo_rows(nq, 8, ZX[1, 32:33, :], 1)
+    for t in (1, 0):
+        wait("w_xm", (not_last, xm_copy[t].wait_recv))
+        with jax.named_scope("c_last"):
+            prep(nx, t, ZX[1, 0:32, :], 3 * nx)
+            acc = pairs([((i, 0, t), (i, 1, t)), ((i, 2, t), (i, 3, t))], acc)
+    comp, vol = acc
 
     row_of = zc * py + gy
 
@@ -610,18 +614,18 @@
         when(has_yl & has_zl, yz_copy.wait_send)
         when(has_zu, zr_copy.wait_send)
         when(has_yu, yu_copy.wait_send)
-        when(plain_down, xm_copy.wait_send, xd_copy.wait_send)
+        when(plain_down, xm_copy[0].wait_send, xm_copy[1].wait_send, xd_copy.wait_send)
         when(plain_down & has_yl, xy_copy.wait_send)
         when(plain_down & has_zl, xz_copy.wait_send)
         when(plain_down & both_l, xyz_copy.wait_send)
-        when(upper0, xm_to_relay.wait_send, xd_to_relay.wait_send)
+        when(upper0, xm_to_relay[0].wait_send, xm_to_relay[1].wait_send, xd_to_relay.wait_send)
         when(upper0 & has_yl & no(skip_y), xy_to_relay.wait_send)
         when(upper0 & has_zl & no(skip_z), xz_to_relay.wait_send)
         when(upper0 & both_l & no(skip_yz), xyz_to_relay.wait_send)
         when(at_corner & has_yu, xy_corner.wait_send)
         when(at_corner & has_zu, xz_corner.wait_send)
         when(at_corner & both_u, xyz_corner.wait_send)
-        when(first_x, xm_relay.wait_send, xd_relay.wait_send)
+        when(first_x, xm_relay[0].wait_send, xm_relay[1].wait_send, xd_relay.wait_send)
         when(first_x & has_yu, xy_relay.wait_send)
         when(first_x & has_zu, xz_relay.wait_send)
         when(first_x & both_u, xyz_relay.wait_send)

time: 39.9 us -> 40.2 us (level)
  no operation moved by 1% of the time
where the time goes in v5:
time: 40.2 us; the launch traced here: 39.7 us
  Pallas kernels  39.1 us (97%)
  between operations  0.64 us (2%)
    pallas_call x1, Pallas kernels, on_device(): pl.pallas_call(functools.partial(kernel, nx, ny, px, py, pz), out_shape=(...  38.2 us
    pallas_call x1, Pallas kernels, on_device(): pl.pallas_call(finish, out_shape=(jax.ShapeDtypeStruct((nx, ny, nz), F32)...  0.83 us

profile of v5, /device:TPU:1, one launch (start us, length us, event | category | flops | bytes accessed | tf_op | source)
XLA Modules:
  0.0 39.7 jit_solution(5034835798614200376)
XLA Ops:
  0.6 38.2 %shard_map.58 = (f32[16,32,256]{2,1,0:T(8,128)S(1)}, f32[8,128]{1,0:T(8,128)S(1)}) custom-call(f32[3,16,32,256]{3,2,1,0:T(8,128)} %disp.1, f32[16,32,256]{2,1,0:T(8,128)} %dens.1, f32[24,24]{1,0:T(8,128)} %stiff.1), custom_call_target="tpu_custom_call" | custom-call | tf_op jit(solution)/shard_map/pallas_call | solution.py:673
  38.9 0.8 %shard_map.59 = (f32[16,32,256]{2,1,0:T(8,128)}, f32[1,1]{1,0:T(1,128)}, f32[1,1]{1,0:T(1,128)}) custom-call(f32[16,32,256]{2,1,0:T(8,128)S(1)} %get-tuple-element.8.out_ref, f32[8,128]{1,0:T(8,128)S(1)} %get-tuple-element.9.sums_ref), custom_call_target="tpu_custom_call" | custom-call | tf_op jit(solution)/shard_map/pallas_call | solution.py:719
